TPU v7x, 256 devices: a whole 4x4x8 slice. The times are simulated.
256 devices in a mesh: dp: 64 (over y, z, core), mp: 4 (over x).
Axes of the slice: x: 4, y: 4, z: 8, core: 2. Of those that a mesh axis runs over, the one named last changes fastest.
Arguments:
- frames: int32 [384], P('dp'), may hold values from 17 to 129, as said below
- owners: int32 [1920], P('dp'), may hold values from -1 to 63, as said below
- offsets: int32 [1920], P('dp'), may hold values from -1 to 17, as said below
- groups: int32 [384], P('dp'), may hold values from 0 to 31, as said below
- latent: bfloat16 [1920, 64, 128], P('dp'), may hold values from -12 to 12
- noise_blocks: bfloat16 [1920, 64, 128], P('dp'), may hold values from -6 to 6
- rewards: float32 [384], P('dp'), may hold values from -6 to 6
- embed_weight: bfloat16 [64, 3072], replicated, may hold values from -2 to 2
- norm_gain: float32 [3072], replicated, may hold values from 0 to 2
- mid_weight: bfloat16 [3072, 3072], P(None, 'mp'), may hold values from -1 to 1
- head_weight: bfloat16 [3072, 64], P('mp'), may hold values from -1 to 1
Outputs:
- prediction: bfloat16 [1152, 64, 128], P('dp')
- log_prob: float32 [384], P('dp')
- advantage: float32 [384], P('dp')
Inputs may be any that keep to these rules, and one draw needn't show every extreme that they name: frames = 4 m + 1 for a whole m; the block counts (frames - 1) // 32 + 1 of all samples add up to exactly 1152, and some rollout device has all its samples at 129 frames. `owners`: a live slot names its owner, an empty one -1; every owner receives exactly 18 blocks; one rollout device sends at most 1 block to one owner, and in every draw some device sends that many to some owner. `offsets`: a live slot's row at its owner, rows distinct at each owner; empty slots -1. `groups`: every prompt has exactly 12 samples.
All inputs are finite; a program needn't handle non-finite values.
Results may differ from a plain program's by a relative error of at most 0.0068.
Values may be sent and summed in bfloat16 or wider, within the bound.
A program may use at most 64 MiB of HBM per device.

v0:
```python
import jax
import jax.numpy as jnp
from jax import lax
from jax.sharding import PartitionSpec as P

MAXB = 5
GSIZE = 12


def copy_for_each(array, axis):
    copies = jnp.broadcast_to(array, (lax.axis_size(axis), *array.shape))
    return lax.all_to_all(copies, axis, split_axis=0, concat_axis=0, tiled=True)


def over_copies(array, axis):
    everything = copy_for_each(array, axis)
    return jnp.sum(everything.astype(jnp.float32), axis=0)


def side_by_side(arrays, axis, split_dim, concat_dim, along):
    widths = [a.shape[along] for a in arrays]
    both = jnp.concatenate(arrays, axis=along)
    whole = lax.all_to_all(both, axis, split_axis=split_dim, concat_axis=concat_dim, tiled=True)
    return tuple(jnp.split(whole, [sum(widths[:k]) for k in range(1, len(widths))], axis=along))


def in_one_piece(arrays, axis, dim, along):
    ends, at = ([], 0)
    for a in arrays[:-1]:
        at += a.shape[along]
        ends.append(at)
    both = jnp.concatenate(arrays, axis=along)
    return tuple(jnp.split(lax.all_gather(both, axis, axis=dim, tiled=True), ends, axis=along))


def taken_together(array, axis):
    return copy_for_each(array, axis).sum(axis=0)


def together(arrays, axis):
    ravelled, at, done = (jnp.concatenate([a.reshape(-1) for a in arrays]), 0, [])
    running = taken_together(ravelled, axis)
    for a in arrays:
        done.append(running[at : at + a.size].reshape(a.shape))
        at += a.size
    return tuple(done)


def forward_blocks(pieces, embed_weight, norm_gain, mid_weight, head_weight):
    latent_part, noise_part = pieces
    embedded = jnp.einsum(
        "nct,cd->ntd", latent_part, embed_weight, preferred_element_type=jnp.float32
    )
    mean_sq = jnp.mean(embedded * embedded, axis=-1, keepdims=True)
    normed = (embedded * lax.rsqrt(mean_sq + 0.25) * norm_gain).astype(jnp.bfloat16)
    mid_out = jnp.einsum("ntd,df->ntf", normed, mid_weight, preferred_element_type=jnp.float32)
    activated = jax.nn.silu(mid_out).astype(jnp.bfloat16)
    partial_head = jnp.einsum(
        "ntf,fc->nct", activated, head_weight, preferred_element_type=jnp.float32
    )
    velocity = over_copies(partial_head.astype(jnp.bfloat16), "mp").astype(jnp.float32)
    errors = noise_part.astype(jnp.float32) + velocity
    return (velocity.astype(jnp.bfloat16), jnp.sum(errors * errors, axis=(1, 2)))


def local(
    frames,
    owners,
    offsets,
    groups,
    latent,
    noise_blocks,
    rewards,
    embed_weight,
    norm_gain,
    mid_weight,
    head_weight,
):
    per_device = frames.shape[0]
    devices = lax.axis_size("dp")
    slot_count = owners.shape[0]
    pair_cap = (slot_count + devices - 1) // devices
    owner_cap = 3 * per_device
    channels = latent.shape[1]
    block_len = latent.shape[2]
    samples = per_device * devices
    counts = (frames - 1) // 32 + 1
    slot_index = jnp.arange(slot_count, dtype=jnp.int32)
    live_slot = slot_index % MAXB < jnp.repeat(counts, MAXB)
    earlier = (
        (owners[:, None] == owners[None, :])
        & live_slot[None, :]
        & (slot_index[None, :] < slot_index[:, None])
    )
    places = jnp.sum(earlier.astype(jnp.int32), axis=1)
    target = jnp.where(live_slot, owners * pair_cap + places, devices * pair_cap)
    sample_ids = lax.axis_index("dp") * per_device + slot_index // MAXB
    meta = jnp.stack(
        [jnp.where(live_slot, offsets, -1), jnp.where(live_slot, sample_ids, -1)], axis=1
    )
    send_meta = jnp.full((devices * pair_cap, 2), -1, jnp.int32).at[target].set(meta, mode="drop")
    part_width = channels // lax.axis_size("mp")
    start = lax.axis_index("mp") * part_width
    latent_src = lax.dynamic_slice_in_dim(latent, start, part_width, 1)
    noise_src = lax.dynamic_slice_in_dim(noise_blocks, start, part_width, 1)
    send_latent = (
        jnp.zeros((devices * pair_cap, part_width, block_len), jnp.bfloat16)
        .at[target]
        .set(latent_src, mode="drop")
    )
    send_noise = (
        jnp.zeros((devices * pair_cap, part_width, block_len), jnp.bfloat16)
        .at[target]
        .set(noise_src, mode="drop")
    )
    recv_latent, recv_noise, recv_meta = (
        *side_by_side((send_latent, send_noise), "dp", 0, 0, 1),
        lax.all_to_all(send_meta, "dp", split_axis=0, concat_axis=0, tiled=True),
    )
    dest_row = jnp.where(recv_meta[:, 0] >= 0, recv_meta[:, 0], owner_cap).astype(jnp.int32)
    owner_latent = (
        jnp.zeros((owner_cap, part_width, block_len), jnp.bfloat16)
        .at[dest_row]
        .set(recv_latent, mode="drop")
    )
    owner_noise = (
        jnp.zeros((owner_cap, part_width, block_len), jnp.bfloat16)
        .at[dest_row]
        .set(recv_noise, mode="drop")
    )
    owner_sample = (
        jnp.full((owner_cap,), -1, jnp.int32).at[dest_row].set(recv_meta[:, 1], mode="drop")
    )
    owner_latent, owner_noise = in_one_piece((owner_latent, owner_noise), "mp", 1, 0)

    def run_group(pieces):
        return forward_blocks(pieces, embed_weight, norm_gain, mid_weight, head_weight)

    grouped = (
        owner_latent.reshape(3, per_device, channels, block_len),
        owner_noise.reshape(3, per_device, channels, block_len),
    )
    preds, slot_sums = lax.map(run_group, grouped)
    prediction = preds.reshape(owner_cap, channels, block_len)
    slot_sums = slot_sums.reshape(owner_cap)
    all_samples = jnp.arange(samples, dtype=jnp.int32)
    per_sample = jnp.sum(
        jnp.where(owner_sample[:, None] == all_samples[None, :], slot_sums[:, None], 0.0), axis=0
    )
    group_count = samples // GSIZE
    in_group = groups[:, None] == jnp.arange(group_count, dtype=jnp.int32)[None, :]
    group_sum = jnp.sum(jnp.where(in_group, rewards[:, None], 0.0), axis=0)
    group_sq = jnp.sum(jnp.where(in_group, (rewards * rewards)[:, None], 0.0), axis=0)
    every_sum, group_sum, group_sq = together((per_sample, group_sum, group_sq), "dp")
    own_sums = lax.dynamic_slice_in_dim(every_sum, lax.axis_index("dp") * per_device, per_device, 0)
    log_prob = -0.5 * own_sums / (counts * block_len * channels).astype(jnp.float32)
    group_mean = group_sum / GSIZE
    variance = group_sq / GSIZE - group_mean * group_mean
    spread = jnp.sqrt(variance + 0.25)
    own_mean = jnp.sum(jnp.where(in_group, group_mean[None, :], 0.0), axis=1)
    own_spread = jnp.sum(jnp.where(in_group, spread[None, :], 0.0), axis=1)
    advantage = (rewards - own_mean) / own_spread
    return (prediction, log_prob, advantage)


def solution(mesh):
    placed = (
        P("dp"),
        P("dp"),
        P("dp"),
        P("dp"),
        P("dp", None, None),
        P("dp", None, None),
        P("dp"),
        P(),
        P(),
        P(None, "mp"),
        P("mp", None),
    )
    return jax.shard_map(
        local,
        mesh=mesh,
        in_specs=placed,
        out_specs=(P("dp", None, None), P("dp"), P("dp")),
        check_vma=False,
    )
```

profile of v0, /device:TPU:1, one launch (start us, length us, event | category | flops | bytes accessed | tf_op | source)
XLA Modules:
  0.0 172.7 jit_solution(12131714856243093316)
XLA Ops:
  2.3 0.9 convert_reduce_fusion.1
  4.0 1.0 constant_dynamic-slice_fusion
  5.0 1.7 scatter_fusion
  6.7 1.7 scatter_fusion.1
  8.4 1.2 scatter_custom_fusion
  9.7 13.1 %all-to-all-start.1 = ((s32[64,1,2]{2,1,0:T(1,128)}), s32[64,1,2]{2,1,0:T(1,128)S(1)}, u32[]{:S(2)}, u32[]{:S(2)}) async-start(s32[64,1,2]{2,1,0:T(1,128)} %bitcast.17), calls=%async_computation.1 | async-start | bytes 65536 | tf_op jit(solution)/shard_map/all_to_all | solution.py:118
  22.8 0.8 pad_maximum_fusion
  23.6 8.4 %all-to-all-done.1 = s32[64,1,2]{2,1,0:T(1,128)S(1)} async-done(((s32[64,1,2]{2,1,0:T(1,128)}), s32[64,1,2]{2,1,0:T(1,128)S(1)}, u32[]{:S(2)}, u32[]{:S(2)}) %all-to-all-start.1) | async-done | bytes 544 | tf_op jit(solution)/shard_map/all_to_all | solution.py:118
  32.0 4.7 %all-to-all-start.2 = ((bf16[64,32,128]{2,1,0:T(8,128)(2,1)}), bf16[64,32,128]{2,1,0:T(8,128)(2,1)S(1)}, u32[]{:S(2)}, u32[]{:S(2)}) async-start(bf16[64,32,128]{2,1,0:T(8,128)(2,1)} %pad_maximum_fusion), calls=%async_computation.2 | async-start | bytes 1048576 | tf_op jit(solution)/shard_map/all_to_all | solution.py:23
  38.3 0.8 scatter_custom_fusion.5
  39.1 14.9 %all-to-all-done.2 = bf16[64,32,128]{2,1,0:T(8,128)(2,1)S(1)} async-done(((bf16[64,32,128]{2,1,0:T(8,128)(2,1)}), bf16[64,32,128]{2,1,0:T(8,128)(2,1)S(1)}, u32[]{:S(2)}, u32[]{:S(2)}) %all-to-all-start.2) | async-done | bytes 524320 | tf_op jit(solution)/shard_map/all_to_all | solution.py:23
  54.1 2.6 %scatter_fusion.2 = bf16[18,16,128]{2,1,0:T(8,128)(2,1)S(1)} fusion(bf16[18,16,128]{2,1,0:T(8,128)(2,1)S(1)} %broadcast.170.clone.1, s32[64]{0:T(128)S(1)} %get-tuple-element.86, bf16[64,16,128]{2,1,0:T(8,128)(2,1)S(1)} %get-tuple-element.81), kind=kCustom, calls=%fused_computation.3 | custom fusion | bytes 786688 | tf_op jit(solution)/shard_map/scatter | solution.py:124
  56.7 2.6 %scatter_fusion.3 = bf16[18,16,128]{2,1,0:T(8,128)(2,1)S(1)} fusion(bf16[18,16,128]{2,1,0:T(8,128)(2,1)S(1)} %broadcast.170.clone, s32[64]{0:T(128)S(1)} %get-tuple-element.86, bf16[64,16,128]{2,1,0:T(8,128)(2,1)S(1)} %get-tuple-element.82), kind=kCustom, calls=%fused_computation.4 | custom fusion | bytes 786688 | tf_op jit(solution)/shard_map/scatter | solution.py:129
  59.3 11.4 %all_gather.3 = bf16[36,64,128]{2,1,0:T(8,128)(2,1)S(1)} all-gather(bf16[36,16,128]{2,1,0:T(8,128)(2,1)S(1)} %pad_maximum_fusion.1), channel_id=1, replica_groups=mesh['dp'=64,'mp'=4] {'mp'}, dimensions={1}, use_global_device_ids=true | all-gather | bytes 737280 | tf_op jit(solution)/shard_map/all_gather | solution.py:33
  70.8 76.3 %while.12 = (s32[]{:T(128)}, bf16[3,6,64,128]{3,2,1,0:T(8,128)(2,1)S(1)}, f32[3,6]{1,0:T(4,128)S(1)}, bf16[3,6,64,128]{3,2,1,0:T(8,128)(2,1)S(1)}, bf16[64,3072]...) while((s32[]{:T(128)}, ...), condition=%wide.region_10.11_spmd, body=%wide.region_6.10_spmd.sunk | while | flops 4016751360 | bytes 27156716 | solution.py:143
  70.9 5.0 %multiply_reduce_fusion.2 = (f32[6,128]{1,0:T(8,128)S(1)}, f32[6,128,3072]{2,1,0:T(8,128)}) fusion(bf16[64,3072]{1,0:T(8,128)(2,1)S(1)} %get-tuple-element.174, bf16[3,6,64,128]{3,2,1,0:T(8,128)(2,1)S(1)} %get-tuple-element.173, s32[]{:T(128)S(6)} %copy.45), kind=kOutput, calls=%fused_computation.7.clone.1 | convolution fusion | flops 306707712 | bytes 9931780 | tf_op jit(solution)/shard_map/while/body/eval_jaxpr/nct,cd->ntd/dot_general | solution.py:51
  75.9 9.6 %fusion.43 = bf16[6,64,128]{2,1,0:T(8,128)(2,1)S(1)} fusion(bf16[3072,768]{1,0:T(8,128)(2,1)} %get-tuple-element.176, f32[6,128,3072]{2,1,0:T(8,128)} %get-tuple-element.146, f32[3072]{0:T(1024)S(1)} %get-tuple-element.175, f32[6,128]{1,0:T(8,128)S(1)} %add_rsqrt_fusion.2, bf16[768,64]{0,1:T(8,128)(2,1)S(1)} %get-tuple-element.177), kind=kOutput, calls=%fused_computation.16.clone.1 | convolution fusion | flops 3709452288 | bytes 14367744 | tf_op jit(solution)/shard_map/while/body/eval_jaxpr/ntf,fc->nct/dot_general | solution.py:58
  85.6 0.8 broadcast_in_dim.136
  86.4 3.5 %all-to-all-start = ((bf16[4,6,64,128]{3,2,1,0:T(8,128)(2,1)}), bf16[4,6,64,128]{3,2,1,0:T(8,128)(2,1)S(1)}, u32[]{:S(2)}, u32[]{:S(2)}) async-start(bf16[4,6,64,128]{3,2,1,0:T(8,128)(2,1)} %broadcast_in_dim.136), calls=%async_computation | async-start | bytes 786432 | tf_op jit(solution)/shard_map/while/body/eval_jaxpr/all_to_all | solution.py:12
  89.8 6.2 %all-to-all-done = bf16[4,6,64,128]{3,2,1,0:T(8,128)(2,1)S(1)} async-done(((bf16[4,6,64,128]{3,2,1,0:T(8,128)(2,1)}), bf16[4,6,64,128]{3,2,1,0:T(8,128)(2,1)S(1)}, u32[]{:S(2)}, u32[]{:S(2)}) %all-to-all-start) | async-done | bytes 393248 | tf_op jit(solution)/shard_map/while/body/eval_jaxpr/all_to_all | solution.py:12
  96.3 5.0 %multiply_reduce_fusion.2 = (f32[6,128]{1,0:T(8,128)S(1)}, f32[6,128,3072]{2,1,0:T(8,128)}) fusion(bf16[64,3072]{1,0:T(8,128)(2,1)S(1)} %get-tuple-element.174, bf16[3,6,64,128]{3,2,1,0:T(8,128)(2,1)S(1)} %get-tuple-element.173, s32[]{:T(128)S(6)} %copy.45), kind=kOutput, calls=%fused_computation.7.clone.1 | convolution fusion | flops 306707712 | bytes 9931780 | tf_op jit(solution)/shard_map/while/body/eval_jaxpr/nct,cd->ntd/dot_general | solution.py:51
  101.4 9.6 %fusion.43 = bf16[6,64,128]{2,1,0:T(8,128)(2,1)S(1)} fusion(bf16[3072,768]{1,0:T(8,128)(2,1)} %get-tuple-element.176, f32[6,128,3072]{2,1,0:T(8,128)} %get-tuple-element.146, f32[3072]{0:T(1024)S(1)} %get-tuple-element.175, f32[6,128]{1,0:T(8,128)S(1)} %add_rsqrt_fusion.2, bf16[768,64]{0,1:T(8,128)(2,1)S(1)} %get-tuple-element.177), kind=kOutput, calls=%fused_computation.16.clone.1 | convolution fusion | flops 3709452288 | bytes 14367744 | tf_op jit(solution)/shard_map/while/body/eval_jaxpr/ntf,fc->nct/dot_general | solution.py:58
  111.0 0.8 broadcast_in_dim.136
  111.8 3.5 %all-to-all-start = ((bf16[4,6,64,128]{3,2,1,0:T(8,128)(2,1)}), bf16[4,6,64,128]{3,2,1,0:T(8,128)(2,1)S(1)}, u32[]{:S(2)}, u32[]{:S(2)}) async-start(bf16[4,6,64,128]{3,2,1,0:T(8,128)(2,1)} %broadcast_in_dim.136), calls=%async_computation | async-start | bytes 786432 | tf_op jit(solution)/shard_map/while/body/eval_jaxpr/all_to_all | solution.py:12
  115.3 6.2 %all-to-all-done = bf16[4,6,64,128]{3,2,1,0:T(8,128)(2,1)S(1)} async-done(((bf16[4,6,64,128]{3,2,1,0:T(8,128)(2,1)}), bf16[4,6,64,128]{3,2,1,0:T(8,128)(2,1)S(1)}, u32[]{:S(2)}, u32[]{:S(2)}) %all-to-all-start) | async-done | bytes 393248 | tf_op jit(solution)/shard_map/while/body/eval_jaxpr/all_to_all | solution.py:12
  121.8 5.0 %multiply_reduce_fusion.2 = (f32[6,128]{1,0:T(8,128)S(1)}, f32[6,128,3072]{2,1,0:T(8,128)}) fusion(bf16[64,3072]{1,0:T(8,128)(2,1)S(1)} %get-tuple-element.174, bf16[3,6,64,128]{3,2,1,0:T(8,128)(2,1)S(1)} %get-tuple-element.173, s32[]{:T(128)S(6)} %copy.45), kind=kOutput, calls=%fused_computation.7.clone.1 | convolution fusion | flops 306707712 | bytes 9931780 | tf_op jit(solution)/shard_map/while/body/eval_jaxpr/nct,cd->ntd/dot_general | solution.py:51
  126.8 9.6 %fusion.43 = bf16[6,64,128]{2,1,0:T(8,128)(2,1)S(1)} fusion(bf16[3072,768]{1,0:T(8,128)(2,1)} %get-tuple-element.176, f32[6,128,3072]{2,1,0:T(8,128)} %get-tuple-element.146, f32[3072]{0:T(1024)S(1)} %get-tuple-element.175, f32[6,128]{1,0:T(8,128)S(1)} %add_rsqrt_fusion.2, bf16[768,64]{0,1:T(8,128)(2,1)S(1)} %get-tuple-element.177), kind=kOutput, calls=%fused_computation.16.clone.1 | convolution fusion | flops 3709452288 | bytes 14367744 | tf_op jit(solution)/shard_map/while/body/eval_jaxpr/ntf,fc->nct/dot_general | solution.py:58
  136.4 0.8 broadcast_in_dim.136
  137.3 3.5 %all-to-all-start = ((bf16[4,6,64,128]{3,2,1,0:T(8,128)(2,1)}), bf16[4,6,64,128]{3,2,1,0:T(8,128)(2,1)S(1)}, u32[]{:S(2)}, u32[]{:S(2)}) async-start(bf16[4,6,64,128]{3,2,1,0:T(8,128)(2,1)} %broadcast_in_dim.136), calls=%async_computation | async-start | bytes 786432 | tf_op jit(solution)/shard_map/while/body/eval_jaxpr/all_to_all | solution.py:12
  140.7 6.2 %all-to-all-done = bf16[4,6,64,128]{3,2,1,0:T(8,128)(2,1)S(1)} async-done(((bf16[4,6,64,128]{3,2,1,0:T(8,128)(2,1)}), bf16[4,6,64,128]{3,2,1,0:T(8,128)(2,1)S(1)}, u32[]{:S(2)}, u32[]{:S(2)}) %all-to-all-start) | async-done | bytes 393248 | tf_op jit(solution)/shard_map/while/body/eval_jaxpr/all_to_all | solution.py:12
  148.2 12.6 %all-to-all-start.3 = ((f32[64,1,448]{2,1,0:T(1,128)}), f32[64,1,448]{2,1,0:T(1,128)S(1)}, u32[]{:S(2)}, u32[]{:S(2)}) async-start(f32[64,1,448]{2,1,0:T(1,128)} %broadcast_in_dim.117), calls=%async_computation.3 | async-start | bytes 262144 | tf_op jit(solution)/shard_map/all_to_all | solution.py:12
  160.8 10.3 %all-to-all-done.3 = f32[64,1,448]{2,1,0:T(1,128)S(1)} async-done(((f32[64,1,448]{2,1,0:T(1,128)}), f32[64,1,448]{2,1,0:T(1,128)S(1)}, u32[]{:S(2)}, u32[]{:S(2)}) %all-to-all-start.3) | async-done | bytes 114720 | tf_op jit(solution)/shard_map/all_to_all | solution.py:12
  (60 shorter events, 7.5 us)
Async XLA Ops:
  0.6 70.2 %copy-start = (bf16[64,3072]{1,0:T(8,128)(2,1)S(1)}, bf16[64,3072]{1,0:T(8,128)(2,1)}, u32[]{:S(2)}) copy-start(bf16[64,3072]{1,0:T(8,128)(2,1)} %param.20) | copy-start | bytes 1179652
  0.6 70.2 %copy-start.6 = (f32[3072]{0:T(1024)S(1)}, f32[3072]{0:T(1024)}, u32[]{:S(2)}) copy-start(f32[3072]{0:T(1024)} %param.21) | copy-start | bytes 36868
  0.7 70.2 %copy-start.5 = (bf16[768,64]{0,1:T(8,128)(2,1)S(1)}, bf16[768,64]{0,1:T(8,128)(2,1)}, u32[]{:S(2)}) copy-start(bf16[768,64]{0,1:T(8,128)(2,1)} %param.23) | copy-start | bytes 294916
  9.7 22.4 %all-to-all-start.1 = ((s32[64,1,2]{2,1,0:T(1,128)}), s32[64,1,2]{2,1,0:T(1,128)S(1)}, u32[]{:S(2)}, u32[]{:S(2)}) async-start(s32[64,1,2]{2,1,0:T(1,128)} %bitcast.17), calls=%async_computation.1 | async-start | bytes 65536 | tf_op jit(solution)/shard_map/all_to_all | solution.py:118
  32.0 22.1 %all-to-all-start.2 = ((bf16[64,32,128]{2,1,0:T(8,128)(2,1)}), bf16[64,32,128]{2,1,0:T(8,128)(2,1)S(1)}, u32[]{:S(2)}, u32[]{:S(2)}) async-start(bf16[64,32,128]{2,1,0:T(8,128)(2,1)} %pad_maximum_fusion), calls=%async_computation.2 | async-start | bytes 1048576 | tf_op jit(solution)/shard_map/all_to_all | solution.py:23
  70.8 100.5 %copy-start.1 = (s32[6]{0:T(128)S(1)}, s32[6]{0:T(128)}, u32[]{:S(2)}) copy-start(s32[6]{0:T(128)} %param.16) | copy-start | bytes 76
  70.8 100.7 %copy-start.2 = (f32[6]{0:T(128)S(1)}, f32[6]{0:T(128)}, u32[]{:S(2)}) copy-start(f32[6]{0:T(128)} %param.19) | copy-start | bytes 76
  70.8 101.2 %copy-start.3 = (s32[6]{0:T(128)S(1)}, s32[6]{0:T(128)}, u32[]{:S(2)}) copy-start(s32[6]{0:T(128)} %param.13) | copy-start | bytes 76
  86.4 9.7 %all-to-all-start = ((bf16[4,6,64,128]{3,2,1,0:T(8,128)(2,1)}), bf16[4,6,64,128]{3,2,1,0:T(8,128)(2,1)S(1)}, u32[]{:S(2)}, u32[]{:S(2)}) async-start(bf16[4,6,64,128]{3,2,1,0:T(8,128)(2,1)} %broadcast_in_dim.136), calls=%async_computation | async-start | bytes 786432 | tf_op jit(solution)/shard_map/while/body/eval_jaxpr/all_to_all | solution.py:12
  111.8 9.7 %all-to-all-start = ((bf16[4,6,64,128]{3,2,1,0:T(8,128)(2,1)}), bf16[4,6,64,128]{3,2,1,0:T(8,128)(2,1)S(1)}, u32[]{:S(2)}, u32[]{:S(2)}) async-start(bf16[4,6,64,128]{3,2,1,0:T(8,128)(2,1)} %broadcast_in_dim.136), calls=%async_computation | async-start | bytes 786432 | tf_op jit(solution)/shard_map/while/body/eval_jaxpr/all_to_all | solution.py:12
  137.3 9.7 %all-to-all-start = ((bf16[4,6,64,128]{3,2,1,0:T(8,128)(2,1)}), bf16[4,6,64,128]{3,2,1,0:T(8,128)(2,1)S(1)}, u32[]{:S(2)}, u32[]{:S(2)}) async-start(bf16[4,6,64,128]{3,2,1,0:T(8,128)(2,1)} %broadcast_in_dim.136), calls=%async_computation | async-start | bytes 786432 | tf_op jit(solution)/shard_map/while/body/eval_jaxpr/all_to_all | solution.py:12
  147.2 25.5 %copy-start.4 = (bf16[3,6,64,128]{3,2,1,0:T(8,128)(2,1)}, bf16[3,6,64,128]{3,2,1,0:T(8,128)(2,1)S(1)}, u32[]{:S(2)}) copy-start(bf16[3,6,64,128]{3,2,1,0:T(8,128)(2,1)S(1)} %get-tuple-element.51) | copy-start | bytes 884740
  148.2 23.0 %all-to-all-start.3 = ((f32[64,1,448]{2,1,0:T(1,128)}), f32[64,1,448]{2,1,0:T(1,128)S(1)}, u32[]{:S(2)}, u32[]{:S(2)}) async-start(f32[64,1,448]{2,1,0:T(1,128)} %broadcast_in_dim.117), calls=%async_computation.3 | async-start | bytes 262144 | tf_op jit(solution)/shard_map/all_to_all | solution.py:12
where the time goes:
time: 173 us
  waiting for transfers between devices  52.3 us (30%)
  matrix products  44 us (25%)
  starting transfers between devices  40.8 us (24%)
  local copies, waits for them, and re-layouts  15.5 us (9%)
  blocking collectives  11.4 us (7%)
  other arithmetic  7.7 us (4%)
    all_to_all x4, waiting for transfers between devices, copy_for_each(): return lax.all_to_all(copies, axis, split_axis=0, concat_axis=0, tiled=True)  28.9 us
    dot_general x3, matrix products, forward_blocks(): jnp.einsum('ntf,fc->nct', activated, head_weight, preferred_element_type=...  28.9 us
    all_to_all x4, starting transfers between devices, copy_for_each(): return lax.all_to_all(copies, axis, split_axis=0, concat_axis=0, tiled=True)  23 us
    dot_general x3, matrix products, forward_blocks(): jnp.einsum('nct,cd->ntd', latent_part, embed_weight, preferred_element_ty...  15.1 us
    all_to_all x1, waiting for transfers between devices, side_by_side(): lax.all_to_all(both, axis, split_axis=split_dim, concat_axis=concat_dim,...  14.9 us
    all_to_all x1, starting transfers between devices, local(): lax.all_to_all(send_meta, 'dp', split_axis=0, concat_axis=0, tiled=True)  13.1 us
    all_gather x1, blocking collectives, in_one_piece(): lax.all_gather(both, axis, axis=dim, tiled=True)  11.4 us
    all_to_all x1, waiting for transfers between devices, local(): lax.all_to_all(send_meta, 'dp', split_axis=0, concat_axis=0, tiled=True)  8.41 us
  transfers between devices with their start and end apart: 6, of which 6 were waited for; matrix products, arithmetic and copies ran while one was open for 2% of the time, Pallas kernels for 0%

commit v1 on v0

v1 whole, which is shorter than its diff:
```python
import functools

import jax
import jax.numpy as jnp
from jax import lax
from jax.experimental import pallas as pl
from jax.experimental.pallas import tpu as pltpu
from jax.sharding import PartitionSpec as P

MESH = pl.DeviceIdType.MESH
D = 3072
C = 64
BT = 128
MAXB = 5
SPD = 6
SLOTS = 30
OB = 18
NY, NZ, NC = 4, 8, 2
NDP = NY * NZ * NC
NMP = 4
F = D // NMP
Q = C // NMP
MCH = 6
MROWS = D // MCH
CHUNKS = 3
CS = SLOTS // CHUNKS
BF = jnp.bfloat16
F32 = jnp.float32


def peer_of(k):
    me = lax.axis_index("dp")
    y, z, c = me // (NZ * NC), (me // NC) % NZ, me % NC
    a = k // (NY * NC)
    dz = NZ // 2 + (1 - 2 * (a % 2)) * ((a + 1) // 2)
    dz = jnp.where(a == NZ - 1, 0, dz)
    b = k % (NY * NC)
    dy = (2 + b // NC) % NY
    dy = jnp.where(b // NC == 2, 3, jnp.where(b // NC == 3, 0, jnp.where(b // NC == 1, 1, 2)))
    dc = 1 - b % NC
    return ((y + dy) % NY) * (NZ * NC) + ((z + dz) % NZ) * NC + (c + dc) % NC


def kernel(
    frames, owners, offsets, groups, rewards,
    gain_h, latent_h, noise_h, embed_h, mid_h, head_h,
    pred_o, logp_o, adv_o,
    ev, gv, mv, hv, lat, noi, av, lw, ht, xs, xr, predb, pay, rcv, rows,
    imeta, fmeta, itab, ftab, stab, invv, invs, idxv, idxs, ext, exr, err,
    in_sem, m_sem, loc_sem, xs_send, xs_recv, meta_send, meta_recv, a2a_send, a2a_recv,
    ag_send, ag_recv, ex_send, ex_recv,
):
    me = lax.axis_index("dp")
    j = lax.axis_index("mp")
    lane = lax.broadcasted_iota(jnp.int32, (8, 128), 1)
    sub = lax.broadcasted_iota(jnp.int32, (8, 128), 0)

    c_e = pltpu.make_async_copy(embed_h, ev, in_sem.at[0])
    c_g = pltpu.make_async_copy(gain_h, gv, in_sem.at[1])
    c_h = pltpu.make_async_copy(head_h, hv, in_sem.at[2])
    c_l = pltpu.make_async_copy(latent_h, lat, in_sem.at[3])
    c_n = pltpu.make_async_copy(noise_h.at[:, pl.ds(pl.multiple_of(j * Q, Q), Q), :], noi, in_sem.at[4])
    c_e.start()
    c_g.start()
    c_m = [
        pltpu.make_async_copy(mid_h.at[pl.ds(k * MROWS, MROWS), :], mv.at[pl.ds(k * MROWS, MROWS), :], m_sem.at[k])
        for k in range(MCH)
    ]
    for c in c_m:
        c.start()
    c_h.start()
    c_l.start()
    c_n.start()

    barrier = pltpu.get_barrier_semaphore()

    def greet(k, _):
        pl.semaphore_signal(barrier, inc=1, device_id=(peer_of(k), j), device_id_type=MESH)
        return 0

    lax.fori_loop(0, NDP - 1, greet, 0)
    for d in range(1, NMP):
        pl.semaphore_signal(barrier, inc=1, device_id=(me, (j + d) % NMP), device_id_type=MESH)

    inv = jnp.zeros((8, 128), jnp.int32)
    off = jnp.full((8, 128), -1, jnp.int32)
    counts = jnp.ones((8, 128), jnp.int32)
    for s in range(SPD):
        n = (frames[s] - 1) // 32 + 1
        counts = jnp.where(sub == s, n, counts)
        for k in range(MAXB):
            slot = s * MAXB + k
            hit = (lane == owners[slot]) & (k < n)
            inv = jnp.where(hit, slot, inv)
            off = jnp.where(hit, offsets[slot], off)
    fm = jnp.zeros((8, 128), F32)
    gown = jnp.full((8, 128), -1, jnp.int32)
    for s in range(SPD):
        off = jnp.where(lane == NDP + s, groups[s], off)
        fm = jnp.where(lane == NDP + s, rewards[s], fm)
        gown = jnp.where(sub == s, groups[s], gown)
    off = jnp.where(lane >= NDP + SPD, -2, off)
    invv[...] = inv
    imeta[...] = off[0:1, :]
    fmeta[...] = fm[0:1, :]
    c_inv = pltpu.make_async_copy(invv, invs, loc_sem.at[0])
    c_inv.start()

    c_e.wait()
    c_g.wait()
    for k in range(D // 128):
        cols = pl.ds(k * 128, 128)
        eg = ev[:, cols].astype(F32) * gv[k : k + 1, :]
        hi = eg.astype(BF)
        av[0:C, cols] = hi
        av[C : 2 * C, cols] = (eg - hi.astype(F32)).astype(BF)
    e = ev[...]
    e4 = jnp.concatenate([e, e, e, e], axis=0)
    gram = lax.dot_general(e, e4, (((1,), (1,)), ((), ())), preferred_element_type=F32)
    g1 = gram.astype(BF).astype(F32)
    g2 = (gram - g1).astype(BF).astype(F32)
    g3 = gram - g1 - g2
    gl = lax.broadcasted_iota(jnp.int32, (C, 4 * C), 1)
    gparts = jnp.where(gl < C, g1, jnp.where(gl < 2 * C, g2, jnp.where(gl < 3 * C, g3, 0.0)))
    lw[F : F + C, :] = gparts.astype(BF)
    w = jnp.zeros((2 * C, F), F32)
    for k in range(MCH):
        c_m[k].wait()
        ks = pl.ds(k * MROWS, MROWS)
        w = w + jnp.dot(av[:, ks], mv[ks, :], preferred_element_type=F32)
    w = w[0:C, :] + w[C : 2 * C, :]
    whi = w.astype(BF).astype(F32)
    wst = jnp.concatenate([whi, w - whi], axis=0)
    lw[0:F, 0 : 2 * C] = jnp.transpose(wst).astype(BF)
    lw[0:F, 2 * C : 4 * C] = jnp.zeros((F, 2 * C), BF)
    c_h.wait()
    eye = (
        lax.broadcasted_iota(jnp.int32, (C, C), 0) == lax.broadcasted_iota(jnp.int32, (C, C), 1)
    ).astype(F32).astype(BF)
    ht[...] = lax.dot_general(eye, hv[...], (((1,), (1,)), ((), ())), preferred_element_type=F32).astype(BF)
    c_l.wait()
    c_n.wait()

    pl.semaphore_wait(barrier, NDP - 1 + NMP - 1)

    def meta_copies(k):
        p = peer_of(k)
        return (
            pltpu.make_async_remote_copy(
                src_ref=imeta, dst_ref=itab.at[me], send_sem=meta_send.at[0], recv_sem=meta_recv.at[0],
                device_id=(p, j), device_id_type=MESH,
            ),
            pltpu.make_async_remote_copy(
                src_ref=fmeta, dst_ref=ftab.at[me], send_sem=meta_send.at[1], recv_sem=meta_recv.at[1],
                device_id=(p, j), device_id_type=MESH,
            ),
        )

    def send_meta(k, _):
        for c in meta_copies(k):
            c.start()
        return 0

    lax.fori_loop(0, NDP - 1, send_meta, 0)
    itab[me] = imeta[...]
    ftab[me] = fmeta[...]

    def xcopy(g, d):
        to = (j + d) % NMP
        sl = pl.ds(g * CS, CS)
        return pltpu.make_async_remote_copy(
            src_ref=xs.at[to, sl], dst_ref=xr.at[d - 1, sl],
            send_sem=xs_send.at[g, d - 1], recv_sem=xs_recv.at[g, d - 1],
            device_id=(me, to), device_id_type=MESH,
        )

    def forward(g, _):
        for p in range(CS // 2):
            s0 = g * CS + 2 * p
            x = jnp.concatenate([lat[s0], lat[s0 + 1]], axis=1)
            x4 = jnp.concatenate([x, x, x, x], axis=0)
            m = jnp.dot(lw[...], x4, preferred_element_type=F32)
            sq = jnp.sum(x.astype(F32) * m[F:, :], axis=0, keepdims=True)
            half = 0.5 * lax.rsqrt(sq * (1.0 / D) + 0.25)
            h = m[:F, :] * half
            act = (h + h * jnp.tanh(h)).astype(BF)
            vel = jnp.dot(ht[...], act, preferred_element_type=F32).astype(BF)
            for q in range(NMP):
                xs[q, s0] = vel[q * Q : (q + 1) * Q, 0:BT]
                xs[q, s0 + 1] = vel[q * Q : (q + 1) * Q, BT : 2 * BT]
        for d in (2, 1, 3):
            xcopy(g, d).start()
        return 0

    lax.fori_loop(0, CHUNKS, forward, 0)
    c_inv.wait()

    def settle(g, _):
        for d in range(1, NMP):
            xcopy(g, d).wait_recv()
        for i in range(CS // MAXB):
            s = g * (CS // MAXB) + i
            n = (frames[s] - 1) // 32 + 1
            acc = jnp.zeros((Q, BT), F32)
            for k in range(MAXB):
                slot = s * MAXB + k
                v = xs[j, slot].astype(F32) + xr[0, slot].astype(F32)
                v = v + (xr[1, slot].astype(F32) + xr[2, slot].astype(F32))
                predb[slot] = v.astype(BF)
                dlt = noi[slot].astype(F32) + v
                acc = acc + jnp.where(k < n, dlt * dlt, 0.0)
            err[s] = jnp.sum(acc, axis=0, keepdims=True)
        return 0

    lax.fori_loop(0, CHUNKS, settle, 0)

    def gather(o, _):
        pay[o] = predb[invs[0, o]]
        return 0

    lax.fori_loop(0, NDP, gather, 0)

    def block_copy(k):
        p = peer_of(k)
        return pltpu.make_async_remote_copy(
            src_ref=pay.at[p], dst_ref=rcv.at[me], send_sem=a2a_send, recv_sem=a2a_recv,
            device_id=(p, j), device_id_type=MESH,
        )

    def send_block(k, _):
        block_copy(k).start()
        return 0

    lax.fori_loop(0, NDP - 1, send_block, 0)
    rcv[me] = pay[me]

    et = jnp.zeros((8, 128), F32)
    for s in range(SPD):
        et = jnp.where(sub == s, err[s], et)
    ext[...] = et
    ex = [
        pltpu.make_async_remote_copy(
            src_ref=ext, dst_ref=exr.at[d - 1], send_sem=ex_send.at[d - 1], recv_sem=ex_recv.at[d - 1],
            device_id=(me, (j + d) % NMP), device_id_type=MESH,
        )
        for d in range(1, NMP)
    ]
    for c in ex:
        c.start()

    def all_of(ref, n, send, recv):
        return pltpu.make_async_remote_copy(
            src_ref=ref.at[pl.ds(0, n)], dst_ref=ref.at[pl.ds(0, n)], send_sem=send, recv_sem=recv,
            device_id=(me, (j + 1) % NMP), device_id_type=MESH,
        )

    all_of(itab, NDP - 1, meta_send.at[0], meta_recv.at[0]).wait_recv()
    all_of(ftab, NDP - 1, meta_send.at[1], meta_recv.at[1]).wait_recv()
    c_tab = pltpu.make_async_copy(itab, stab, loc_sem.at[1])
    c_tab.start()

    def prompt(s, carry):
        a, b = carry
        hit = gown == itab[s]
        r = jnp.where(hit & (lane >= NDP), jnp.broadcast_to(ftab[s], (8, 128)), 0.0)
        return a + r, b + r * r

    zero = jnp.zeros((8, 128), F32)
    gsum, gsq = lax.fori_loop(0, NDP, prompt, (zero, zero))
    mean = jnp.sum(gsum, axis=1, keepdims=True) * (1.0 / 12.0)
    var = jnp.sum(gsq, axis=1, keepdims=True) * (1.0 / 12.0) - mean * mean
    own = jnp.zeros((8, 128), F32)
    for s in range(SPD):
        own = jnp.where(sub == s, rewards[s], own)
    adv = (own - mean) / jnp.sqrt(var + 0.25)
    adv_o[...] = jnp.sum(jnp.where(lane == sub, adv, 0.0), axis=0, keepdims=True)

    c_tab.wait()

    def place(s, acc):
        return jnp.where(lane == stab[s, 0, me], s, acc)

    idxv[...] = lax.fori_loop(0, NDP, place, jnp.zeros((8, 128), jnp.int32))
    c_idx = pltpu.make_async_copy(idxv, idxs, loc_sem.at[2])
    c_idx.start()
    c_idx.wait()

    for c in ex:
        c.wait_recv()
    tot = jnp.sum(ext[...] + exr[0] + (exr[1] + exr[2]), axis=1, keepdims=True)
    lp = -0.5 * tot / (counts * (BT * C)).astype(F32)
    logp_o[...] = jnp.sum(jnp.where(lane == sub, lp, 0.0), axis=0, keepdims=True)

    all_of(rcv, NDP - 1, a2a_send, a2a_recv).wait_recv()

    def place_row(r, _):
        rows[r] = rcv[idxs[0, r]]
        return 0

    lax.fori_loop(0, OB, place_row, 0)
    ch = pl.ds(pl.multiple_of(j * Q, Q), Q)
    ag = [
        pltpu.make_async_remote_copy(
            src_ref=rows, dst_ref=pred_o.at[:, ch, :], send_sem=ag_send.at[d - 1], recv_sem=ag_recv.at[d - 1],
            device_id=(me, (j + d) % NMP), device_id_type=MESH,
        )
        for d in (2, 1, 3)
    ]
    for c in ag:
        c.start()
    c_own = pltpu.make_async_copy(rows, pred_o.at[:, ch, :], loc_sem.at[3])
    c_own.start()

    all_of(itab, NDP - 1, meta_send.at[0], meta_recv.at[0]).wait_send()
    all_of(ftab, NDP - 1, meta_send.at[1], meta_recv.at[1]).wait_send()
    all_of(rcv, NDP - 1, a2a_send, a2a_recv).wait_send()

    def drain(g, _):
        for d in range(1, NMP):
            xcopy(g, d).wait_send()
        return 0

    lax.fori_loop(0, CHUNKS, drain, 0)
    for c in ex:
        c.wait_send()
    c_own.wait()
    for c in ag:
        c.wait()


def local(
    frames, owners, offsets, groups, latent, noise_blocks, rewards, embed_weight, norm_gain, mid_weight, head_weight
):
    smem = pl.BlockSpec(memory_space=pltpu.SMEM)
    hbm = pl.BlockSpec(memory_space=pl.ANY)
    vmem = pl.BlockSpec(memory_space=pltpu.VMEM)
    dma = pltpu.SemaphoreType.DMA
    V = pltpu.VMEM
    scratch = [
        V((C, D), BF), V((D // 128, 128), F32), V((D, F), BF), V((F, C), BF),
        V((SLOTS, C, BT), BF), V((SLOTS, Q, BT), BF),
        V((2 * C, D), BF), V((F + C, 4 * C), BF), V((C, F), BF),
        V((NMP, SLOTS, Q, BT), BF), V((NMP - 1, SLOTS, Q, BT), BF),
        V((SLOTS, Q, BT), BF), V((NDP, Q, BT), BF), V((NDP, Q, BT), BF), V((OB, Q, BT), BF),
        V((1, 128), jnp.int32), V((1, 128), F32), V((NDP, 1, 128), jnp.int32), V((NDP, 1, 128), F32),
        pltpu.SMEM((NDP, 1, 128), jnp.int32),
        V((8, 128), jnp.int32), pltpu.SMEM((8, 128), jnp.int32),
        V((8, 128), jnp.int32), pltpu.SMEM((8, 128), jnp.int32),
        V((8, 128), F32), V((NMP - 1, 8, 128), F32), V((SPD, 1, 128), F32),
        dma((5,)), dma((MCH,)), dma((4,)),
        dma((CHUNKS, NMP - 1)), dma((CHUNKS, NMP - 1)),
        dma((2,)), dma((2,)), dma, dma,
        dma((NMP - 1,)), dma((NMP - 1,)), dma((NMP - 1,)), dma((NMP - 1,)),
    ]
    pred, logp, adv = pl.pallas_call(
        kernel,
        out_shape=(
            jax.ShapeDtypeStruct((OB, C, BT), BF),
            jax.ShapeDtypeStruct((1, 128), F32),
            jax.ShapeDtypeStruct((1, 128), F32),
        ),
        in_specs=[smem] * 5 + [hbm] * 6,
        out_specs=(hbm, vmem, vmem),
        scratch_shapes=scratch,
        compiler_params=pltpu.CompilerParams(
            collective_id=0, has_side_effects=True, vmem_limit_bytes=48 * 1024 * 1024
        ),
        name="regroup_forward",
    )(
        frames, owners, offsets, groups, rewards,
        norm_gain.reshape(D // 128, 128), latent, noise_blocks, embed_weight, mid_weight, head_weight,
    )
    return pred, logp[0, :SPD], adv[0, :SPD]


def solution(mesh):
    placed = (
        P("dp"), P("dp"), P("dp"), P("dp"), P("dp", None, None), P("dp", None, None), P("dp"),
        P(), P(), P(None, "mp"), P("mp", None),
    )
    return jax.shard_map(
        local,
        mesh=mesh,
        in_specs=placed,
        out_specs=(P("dp", None, None), P("dp"), P("dp")),
        check_vma=False,
    )
```

time: 173 us -> 56.2 us (0.32)
  waiting for transfers between devices: 52.3 us -> 0 us
  Pallas kernels: 0 us -> 45.9 us
  matrix products: 44 us -> 0 us
  starting transfers between devices: 40.8 us -> 0 us
  blocking collectives: 11.4 us -> 0 us
  other arithmetic: 7.7 us -> 0 us
  local copies, waits for them, and re-layouts: 15.5 us -> 9.32 us
    all_to_all x6 -> x0, waiting for transfers between devices: 52.3 us -> none  [the longest x4 28.9 us: copy_for_each(): return lax.all_to_all(copies, axis, split_axis=0, concat_axis=0, tiled=True)]
    pallas_call x0 -> x1, Pallas kernels: none -> 45.9 us  [local(): pl.pallas_call(kernel, out_shape=(jax.ShapeDtypeStruct((OB, C, BT), BF),...]
    dot_general x6 -> x0, matrix products: 44 us -> none  [the longest x3 28.9 us: forward_blocks(): jnp.einsum('ntf,fc->nct', activated, head_weight, preferred_element_type=...]
    all_to_all x6 -> x0, starting transfers between devices: 40.8 us -> none  [the longest x4 23 us: copy_for_each(): return lax.all_to_all(copies, axis, split_axis=0, concat_axis=0, tiled=True)]
    all_gather x1 -> x0, blocking collectives: 11.4 us -> none  [in_one_piece(): lax.all_gather(both, axis, axis=dim, tiled=True)]
    scatter x6 -> x0, local copies, waits for them, and re-layouts: 10.5 us -> none  [the longest x1 2.58 us: local(): owner_latent = jnp.zeros((owner_cap, part_width, block_len), jnp.bfloat16...]
    unnamed x14 -> x20, local copies, waits for them, and re-layouts: 0.04 us -> 8.8 us
    broadcast_in_dim x6 -> x0, local copies, waits for them, and re-layouts: 3.33 us -> none  [the longest x4 3.18 us: copy_for_each(): copies = jnp.broadcast_to(array, (lax.axis_size(axis), *array.shape))]
  transfers between devices with their start and end apart: 6 -> 0, of which waited for: 6 -> 0; matrix products, arithmetic and copies ran while one was open for 2% -> 0% of each run, Pallas kernels for 0% -> 0%
where the time goes in v1:
time: 56.2 us; the launch traced here: 55.8 us
  Pallas kernels  45.9 us (82%)
  local copies, waits for them, and re-layouts  9.32 us (17%)
  between operations  0.66 us (1%)
    pallas_call x1, Pallas kernels, local(): pl.pallas_call(kernel, out_shape=(jax.ShapeDtypeStruct((OB, C, BT), BF),...  45.9 us
    unnamed x20, local copies, waits for them, and re-layouts  8.8 us

profile of v1, /device:TPU:1, one launch (start us, length us, event | category | flops | bytes accessed | tf_op | source)
XLA Modules:
  0.0 55.8 jit_solution(2433549769869299123)
XLA Ops:
  0.6 1.1 %copy.14.head_h = bf16[768,64]{1,0:T(8,128)(2,1)S(1)} copy(bf16[768,64]{0,1:T(8,128)(2,1)} %param.21) | data formatting | bytes 196608 | tf_op args[10]
  1.7 0.0 copy-start
  1.7 1.0 %copy-done = bf16[30,64,128]{2,1,0:T(8,128)(2,1)S(1)} copy-done((bf16[30,64,128]{2,1,0:T(8,128)(2,1)S(1)}, bf16[30,64,128]{2,1,0:T(8,128)(2,1)}, u32[]{:S(2)}) %copy-start) | copy-done | bytes 491544
  2.7 0.0 copy-start.1
  2.7 1.0 %copy-done.1 = bf16[30,64,128]{2,1,0:T(8,128)(2,1)S(1)} copy-done((bf16[30,64,128]{2,1,0:T(8,128)(2,1)S(1)}, bf16[30,64,128]{2,1,0:T(8,128)(2,1)}, u32[]{:S(2)}) %copy-start.1) | copy-done | bytes 491544
  3.8 0.0 copy-start.2
  3.8 1.0 %copy-done.2 = bf16[64,3072]{1,0:T(8,128)(2,1)S(1)} copy-done((bf16[64,3072]{1,0:T(8,128)(2,1)S(1)}, bf16[64,3072]{1,0:T(8,128)(2,1)}, u32[]{:S(2)}) %copy-start.2) | copy-done | bytes 393240
  4.8 0.0 copy-start.3
  4.8 0.7 %copy-done.3 = f32[3072]{0:T(1024)S(1)} copy-done((f32[3072]{0:T(1024)S(1)}, f32[3072]{0:T(1024)}, u32[]{:S(2)}) %copy-start.3) | copy-done | bytes 12312
  5.5 0.0 copy-start.4
  5.5 0.7 %copy-done.4 = s32[6]{0:T(128)S(1)} copy-done((s32[6]{0:T(128)S(1)}, s32[6]{0:T(128)}, u32[]{:S(2)}) %copy-start.4) | copy-done | bytes 48
  6.1 0.0 copy-start.5
  6.1 0.7 %copy-done.5 = s32[30]{0:T(128)S(1)} copy-done((s32[30]{0:T(128)S(1)}, s32[30]{0:T(128)}, u32[]{:S(2)}) %copy-start.5) | copy-done | bytes 144
  6.8 0.0 copy-start.6
  6.8 0.7 %copy-done.6 = s32[30]{0:T(128)S(1)} copy-done((s32[30]{0:T(128)S(1)}, s32[30]{0:T(128)}, u32[]{:S(2)}) %copy-start.6) | copy-done | bytes 144
  7.4 0.0 copy-start.7
  7.4 0.7 %copy-done.7 = s32[6]{0:T(128)S(1)} copy-done((s32[6]{0:T(128)S(1)}, s32[6]{0:T(128)}, u32[]{:S(2)}) %copy-start.7) | copy-done | bytes 48
  8.1 0.0 copy-start.8
  8.1 0.7 %copy-done.8 = f32[6]{0:T(128)S(1)} copy-done((f32[6]{0:T(128)S(1)}, f32[6]{0:T(128)}, u32[]{:S(2)}) %copy-start.8) | copy-done | bytes 48
  8.7 45.9 %regroup_forward.1 = (bf16[18,64,128]{2,1,0:T(8,128)(2,1)S(1)}, f32[1,128]{1,0:T(1,128)S(1)}, f32[1,128]{1,0:T(1,128)S(1)}) custom-call(s32[6]{0:T(128)S(1)} %copy-done.4, s32[30]{0:T(128)S(1)} %copy-done.5, s32[30]{0:T(128)S(1)} %copy-done.6, s32[6]{0:T(128)S(1)} %copy-done.7, f32[6]{0:T(128)S(1)} %copy-done.8, f32[24,128]{1,0:T(8,128)S(1)} %bitcast.5, ...), custom_call_target="tpu_custom_call" | custom-call | tf_op jit(solution)/shard_map/regroup_forward/pallas_call | solution.py:355
  54.6 0.5 slice_bitcast_fusion
  55.1 0.7 %copy.16 = bf16[18,64,128]{2,1,0:T(8,128)(2,1)} copy(bf16[18,64,128]{2,1,0:T(8,128)(2,1)S(1)} %get-tuple-element.14) | data formatting | bytes 589824
Async XLA Ops:
  1.7 1.0 %copy-start = (bf16[30,64,128]{2,1,0:T(8,128)(2,1)S(1)}, bf16[30,64,128]{2,1,0:T(8,128)(2,1)}, u32[]{:S(2)}) copy-start(bf16[30,64,128]{2,1,0:T(8,128)(2,1)} %latent_h.1) | copy-start | bytes 1474564
  2.7 1.0 %copy-start.1 = (bf16[30,64,128]{2,1,0:T(8,128)(2,1)S(1)}, bf16[30,64,128]{2,1,0:T(8,128)(2,1)}, u32[]{:S(2)}) copy-start(bf16[30,64,128]{2,1,0:T(8,128)(2,1)} %noise_h.1) | copy-start | bytes 1474564
  3.8 1.0 %copy-start.2 = (bf16[64,3072]{1,0:T(8,128)(2,1)S(1)}, bf16[64,3072]{1,0:T(8,128)(2,1)}, u32[]{:S(2)}) copy-start(bf16[64,3072]{1,0:T(8,128)(2,1)} %embed_h.1) | copy-start | bytes 1179652
  4.8 0.7 %copy-start.3 = (f32[3072]{0:T(1024)S(1)}, f32[3072]{0:T(1024)}, u32[]{:S(2)}) copy-start(f32[3072]{0:T(1024)} %param.19) | copy-start | bytes 36868
  5.5 0.7 %copy-start.4 = (s32[6]{0:T(128)S(1)}, s32[6]{0:T(128)}, u32[]{:S(2)}) copy-start(s32[6]{0:T(128)} %frames.1) | copy-start | bytes 76
  6.1 0.7 %copy-start.5 = (s32[30]{0:T(128)S(1)}, s32[30]{0:T(128)}, u32[]{:S(2)}) copy-start(s32[30]{0:T(128)} %owners.1) | copy-start | bytes 364
  6.8 0.7 %copy-start.6 = (s32[30]{0:T(128)S(1)}, s32[30]{0:T(128)}, u32[]{:S(2)}) copy-start(s32[30]{0:T(128)} %offsets.1) | copy-start | bytes 364
  7.4 0.7 %copy-start.7 = (s32[6]{0:T(128)S(1)}, s32[6]{0:T(128)}, u32[]{:S(2)}) copy-start(s32[6]{0:T(128)} %groups.1) | copy-start | bytes 76
  8.1 0.7 %copy-start.8 = (f32[6]{0:T(128)S(1)}, f32[6]{0:T(128)}, u32[]{:S(2)}) copy-start(f32[6]{0:T(128)} %rewards.1) | copy-start | bytes 76

commit v2 on v1

v2 whole, which is shorter than its diff:
```python
import functools

import jax
import jax.numpy as jnp
from jax import lax
from jax.experimental import pallas as pl
from jax.experimental.pallas import tpu as pltpu
from jax.sharding import PartitionSpec as P

MESH = pl.DeviceIdType.MESH
D = 3072
C = 64
BT = 128
MAXB = 5
SPD = 6
SLOTS = 30
OB = 18
NY, NZ, NC = 4, 8, 2
NDP = NY * NZ * NC
NMP = 4
F = D // NMP
Q = C // NMP
MCH = 6
MROWS = D // MCH
CHUNKS = 3
CS = SLOTS // CHUNKS
BF = jnp.bfloat16
F32 = jnp.float32


def peer_of(k):
    return (lax.axis_index("dp") + 1 + (k + 7) % (NDP - 1)) % NDP


def kernel(
    frames_h, owners_h, offsets_h, groups_h, rewards_h,
    gain_h, latent_h, noise_h, embed_h, mid_h, head_h,
    pred_o, logp_o, adv_o,
    frames, owners, offsets, groups, rewards,
    ev, gv, mv, lat, noi, av, lw, ht, mb0, mb1, xs, xr, predb, pay, rcv, rows,
    imeta, fmeta, itab, ftab, stab, invv, invs, idxv, idxs, ext, exr, err,
    in_sem, s_sem, m_sem, loc_sem, xs_send, xs_recv, meta_send, meta_recv, a2a_send, a2a_recv,
    ag_send, ag_recv, ex_send, ex_recv,
):
    me = lax.axis_index("dp")
    j = lax.axis_index("mp")
    barrier = pltpu.get_barrier_semaphore()

    c_e = pltpu.make_async_copy(embed_h, ev, in_sem.at[0])
    c_g = pltpu.make_async_copy(gain_h, gv, in_sem.at[1])
    c_h = pltpu.make_async_copy(head_h, ht, in_sem.at[2])
    c_l = pltpu.make_async_copy(latent_h, lat, in_sem.at[3])
    c_n = pltpu.make_async_copy(noise_h.at[:, pl.ds(pl.multiple_of(j * Q, Q), Q), :], noi, in_sem.at[4])
    c_m = [
        pltpu.make_async_copy(mid_h.at[pl.ds(k * MROWS, MROWS), :], mv.at[pl.ds(k * MROWS, MROWS), :], m_sem.at[k])
        for k in range(MCH)
    ]
    c_s = [
        pltpu.make_async_copy(src, dst, s_sem.at[k])
        for k, (src, dst) in enumerate(
            ((frames_h, frames), (owners_h, owners), (offsets_h, offsets), (groups_h, groups), (rewards_h, rewards))
        )
    ]
    c_e.start()
    c_g.start()
    for c in c_m:
        c.start()
    c_l.start()
    c_h.start()
    c_n.start()
    for c in c_s:
        c.start()

    for k in range(NDP - 1):
        pl.semaphore_signal(barrier, inc=1, device_id=(peer_of(k), j), device_id_type=MESH)
    for d in range(1, NMP):
        pl.semaphore_signal(barrier, inc=1, device_id=(me, (j + d) % NMP), device_id_type=MESH)

    with jax.named_scope("prep"):
        c_e.wait()
        c_g.wait()
        for k in range(D // 128):
            cols = pl.ds(k * 128, 128)
            eg = ev[:, cols].astype(F32) * gv[k : k + 1, :]
            hi = eg.astype(BF)
            av[0:C, cols] = hi
            av[C : 2 * C, cols] = (eg - hi.astype(F32)).astype(BF)
        e = ev[...]
        e4 = jnp.concatenate([e, e, e, e], axis=0)
        gram = lax.dot_general(e, e4, (((1,), (1,)), ((), ())), preferred_element_type=F32)
        g1 = gram.astype(BF).astype(F32)
        g2 = (gram - g1).astype(BF).astype(F32)
        g3 = gram - g1 - g2
        gl = lax.broadcasted_iota(jnp.int32, (C, 4 * C), 1)
        gparts = jnp.where(gl < C, g1, jnp.where(gl < 2 * C, g2, jnp.where(gl < 3 * C, g3, 0.0)))
        lw[F : F + C, :] = gparts.astype(BF)
        w = jnp.zeros((2 * C, F), F32)
        for k in range(MCH):
            c_m[k].wait()
            ks = pl.ds(k * MROWS, MROWS)
            w = w + jnp.dot(av[:, ks], mv[ks, :], preferred_element_type=F32)
        w = w[0:C, :] + w[C : 2 * C, :]
        whi = w.astype(BF).astype(F32)
        wst = jnp.concatenate([whi, w - whi], axis=0)
        lw[0:F, 0 : 2 * C] = jnp.transpose(wst).astype(BF)
        lw[0:F, 2 * C : 4 * C] = jnp.zeros((F, 2 * C), BF)
        c_l.wait()
        c_h.wait()

    def xcopy(g, d):
        to = (j + d) % NMP
        sl = pl.ds(g * CS, CS)
        return pltpu.make_async_remote_copy(
            src_ref=xs.at[to, sl], dst_ref=xr.at[d - 1, sl],
            send_sem=xs_send.at[g, d - 1], recv_sem=xs_recv.at[g, d - 1],
            device_id=(me, to), device_id_type=MESH,
        )

    def pair(p):
        return jnp.concatenate([lat[2 * p], lat[2 * p + 1]], axis=1)

    def project(p, mb):
        x = pair(p)
        x4 = jnp.concatenate([x, x, x, x], axis=0)
        mb[...] = jnp.dot(lw[...], x4, preferred_element_type=F32)

    def finish(p, mb):
        sq = jnp.sum(pair(p).astype(F32) * mb[F:, :], axis=0, keepdims=True)
        half = 0.5 * lax.rsqrt(sq * (1.0 / D) + 0.25)
        h = mb[:F, :] * half
        act = (h + h * jnp.tanh(h)).astype(BF)
        vel = jnp.dot(ht[...], act, preferred_element_type=F32).astype(BF)
        for q in range(NMP):
            xs[q, 2 * p] = vel[q * Q : (q + 1) * Q, 0:BT]
            xs[q, 2 * p + 1] = vel[q * Q : (q + 1) * Q, BT : 2 * BT]

    mbs = (mb0, mb1)
    with jax.named_scope("forward"):
        project(0, mb0)
        for p in range(SLOTS // 2):
            if p + 1 < SLOTS // 2:
                project(p + 1, mbs[(p + 1) % 2])
            finish(p, mbs[p % 2])
            if (2 * p + 2) % CS == 0:
                if (2 * p + 2) // CS == 1:
                    pl.semaphore_wait(barrier, NDP - 1 + NMP - 1)
                for d in (2, 1, 3):
                    xcopy((2 * p + 2) // CS - 1, d).start()

    lane = lax.broadcasted_iota(jnp.int32, (8, 128), 1)
    sub = lax.broadcasted_iota(jnp.int32, (8, 128), 0)
    with jax.named_scope("meta"):
        for c in c_s:
            c.wait()
        inv = jnp.zeros((8, 128), jnp.int32)
        off = jnp.full((8, 128), -1, jnp.int32)
        counts = jnp.ones((8, 128), jnp.int32)
        fm = jnp.zeros((8, 128), F32)
        gown = jnp.full((8, 128), -1, jnp.int32)
        own = jnp.zeros((8, 128), F32)
        for s in range(SPD):
            n = (frames[s] - 1) // 32 + 1
            counts = jnp.where(sub == s, n, counts)
            for k in range(MAXB):
                slot = s * MAXB + k
                hit = (lane == owners[slot]) & (k < n)
                inv = jnp.where(hit, slot, inv)
                off = jnp.where(hit, offsets[slot], off)
            off = jnp.where(lane == NDP + s, groups[s], off)
            fm = jnp.where(lane == NDP + s, rewards[s], fm)
            gown = jnp.where(sub == s, groups[s], gown)
            own = jnp.where(sub == s, rewards[s], own)
        off = jnp.where(lane >= NDP + SPD, -2, off)
        invv[...] = inv
        imeta[...] = off[0:1, :]
        fmeta[...] = fm[0:1, :]
        itab[me] = off[0:1, :]
        ftab[me] = fm[0:1, :]
        c_inv = pltpu.make_async_copy(invv, invs, loc_sem.at[0])
        c_inv.start()

        def send_meta(k, _):
            p = peer_of(k)
            for i, (src, tab) in enumerate(((imeta, itab), (fmeta, ftab))):
                pltpu.make_async_remote_copy(
                    src_ref=src, dst_ref=tab.at[me], send_sem=meta_send.at[i], recv_sem=meta_recv.at[i],
                    device_id=(p, j), device_id_type=MESH,
                ).start()
            return 0

        lax.fori_loop(0, NDP - 1, send_meta, 0)
        c_n.wait()

    with jax.named_scope("settle"):
        for g in range(CHUNKS):
            for d in range(1, NMP):
                xcopy(g, d).wait_recv()
            for i in range(CS // MAXB):
                s = g * (CS // MAXB) + i
                n = (frames[s] - 1) // 32 + 1
                acc = jnp.zeros((Q, BT), F32)
                for k in range(MAXB):
                    slot = s * MAXB + k
                    v = xs[j, slot].astype(F32) + xr[0, slot].astype(F32)
                    v = v + (xr[1, slot].astype(F32) + xr[2, slot].astype(F32))
                    predb[slot] = v.astype(BF)
                    dlt = noi[slot].astype(F32) + v
                    acc = acc + jnp.where(k < n, dlt * dlt, 0.0)
                err[s] = jnp.sum(acc, axis=0, keepdims=True)
        c_inv.wait()

    with jax.named_scope("gather"):
        for o in range(NDP):
            pay[o] = predb[invs[0, o]]

    def send_block(k, _):
        p = peer_of(k)
        pltpu.make_async_remote_copy(
            src_ref=pay.at[p], dst_ref=rcv.at[me], send_sem=a2a_send, recv_sem=a2a_recv,
            device_id=(p, j), device_id_type=MESH,
        ).start()
        return 0

    with jax.named_scope("send_block"):
        lax.fori_loop(0, NDP - 1, send_block, 0)
        rcv[me] = pay[me]

    et = jnp.zeros((8, 128), F32)
    for s in range(SPD):
        et = jnp.where(sub == s, err[s], et)
    ext[...] = et
    ex = [
        pltpu.make_async_remote_copy(
            src_ref=ext, dst_ref=exr.at[d - 1], send_sem=ex_send.at[d - 1], recv_sem=ex_recv.at[d - 1],
            device_id=(me, (j + d) % NMP), device_id_type=MESH,
        )
        for d in range(1, NMP)
    ]
    for c in ex:
        c.start()

    def all_of(ref, n, send, recv):
        return pltpu.make_async_remote_copy(
            src_ref=ref.at[pl.ds(0, n)], dst_ref=ref.at[pl.ds(0, n)], send_sem=send, recv_sem=recv,
            device_id=(me, (j + 1) % NMP), device_id_type=MESH,
        )

    with jax.named_scope("tables"):
        all_of(itab, NDP - 1, meta_send.at[0], meta_recv.at[0]).wait_recv()
        all_of(ftab, NDP - 1, meta_send.at[1], meta_recv.at[1]).wait_recv()
        c_tab = pltpu.make_async_copy(itab, stab, loc_sem.at[1])
        c_tab.start()

        def prompt(s, carry):
            a, b = carry
            hit = gown == itab[s]
            r = jnp.where(hit & (lane >= NDP), jnp.broadcast_to(ftab[s], (8, 128)), 0.0)
            return a + r, b + r * r

        zero = jnp.zeros((8, 128), F32)
        gsum, gsq = lax.fori_loop(0, NDP, prompt, (zero, zero))
        mean = jnp.sum(gsum, axis=1, keepdims=True) * (1.0 / 12.0)
        var = jnp.sum(gsq, axis=1, keepdims=True) * (1.0 / 12.0) - mean * mean
        adv = (own - mean) / jnp.sqrt(var + 0.25)
        adv_o[...] = jnp.sum(jnp.where(lane == sub, adv, 0.0), axis=0, keepdims=True)
        c_tab.wait()
        idx = jnp.zeros((8, 128), jnp.int32)
        for s in range(NDP):
            idx = jnp.where(lane == stab[s, 0, me], s, idx)
        idxv[...] = idx
        c_idx = pltpu.make_async_copy(idxv, idxs, loc_sem.at[2])
        c_idx.start()
        c_idx.wait()
        for c in ex:
            c.wait_recv()
        tot = jnp.sum(ext[...] + exr[0] + (exr[1] + exr[2]), axis=1, keepdims=True)
        lp = -0.5 * tot / (counts * (BT * C)).astype(F32)
        logp_o[...] = jnp.sum(jnp.where(lane == sub, lp, 0.0), axis=0, keepdims=True)

    with jax.named_scope("a2a_wait"):
        all_of(rcv, NDP - 1, a2a_send, a2a_recv).wait_recv()
    for r in range(OB):
        rows[r] = rcv[idxs[0, r]]
    ch = pl.ds(pl.multiple_of(j * Q, Q), Q)
    ag = [
        pltpu.make_async_remote_copy(
            src_ref=rows, dst_ref=pred_o.at[:, ch, :], send_sem=ag_send.at[d - 1], recv_sem=ag_recv.at[d - 1],
            device_id=(me, (j + d) % NMP), device_id_type=MESH,
        )
        for d in (2, 1, 3)
    ]
    for c in ag:
        c.start()
    c_own = pltpu.make_async_copy(rows, pred_o.at[:, ch, :], loc_sem.at[3])
    c_own.start()

    with jax.named_scope("final_wait"):
        all_of(itab, NDP - 1, meta_send.at[0], meta_recv.at[0]).wait_send()
        all_of(ftab, NDP - 1, meta_send.at[1], meta_recv.at[1]).wait_send()
        all_of(rcv, NDP - 1, a2a_send, a2a_recv).wait_send()
        for g in range(CHUNKS):
            for d in range(1, NMP):
                xcopy(g, d).wait_send()
        for c in ex:
            c.wait_send()
        c_own.wait()
        for c in ag:
            c.wait()


def local(
    frames, owners, offsets, groups, latent, noise_blocks, rewards, embed_weight, norm_gain, mid_weight, head_weight
):
    hbm = pl.BlockSpec(memory_space=pl.ANY)
    vmem = pl.BlockSpec(memory_space=pltpu.VMEM)
    dma = pltpu.SemaphoreType.DMA
    V = pltpu.VMEM
    S = pltpu.SMEM
    scratch = [
        S((SPD,), jnp.int32), S((SLOTS,), jnp.int32), S((SLOTS,), jnp.int32), S((SPD,), jnp.int32), S((SPD,), F32),
        V((C, D), BF), V((D // 128, 128), F32), V((D, F), BF),
        V((SLOTS, C, BT), BF), V((SLOTS, Q, BT), BF),
        V((2 * C, D), BF), V((F + C, 4 * C), BF), V((C, F), BF), V((F + C, 2 * BT), F32), V((F + C, 2 * BT), F32),
        V((NMP, SLOTS, Q, BT), BF), V((NMP - 1, SLOTS, Q, BT), BF),
        V((SLOTS, Q, BT), BF), V((NDP, Q, BT), BF), V((NDP, Q, BT), BF), V((OB, Q, BT), BF),
        V((1, 128), jnp.int32), V((1, 128), F32), V((NDP, 1, 128), jnp.int32), V((NDP, 1, 128), F32),
        pltpu.SMEM((NDP, 1, 128), jnp.int32),
        V((8, 128), jnp.int32), pltpu.SMEM((8, 128), jnp.int32),
        V((8, 128), jnp.int32), pltpu.SMEM((8, 128), jnp.int32),
        V((8, 128), F32), V((NMP - 1, 8, 128), F32), V((SPD, 1, 128), F32),
        dma((5,)), dma((5,)), dma((MCH,)), dma((4,)),
        dma((CHUNKS, NMP - 1)), dma((CHUNKS, NMP - 1)),
        dma((2,)), dma((2,)), dma, dma,
        dma((NMP - 1,)), dma((NMP - 1,)), dma((NMP - 1,)), dma((NMP - 1,)),
    ]
    pred, logp, adv = pl.pallas_call(
        kernel,
        out_shape=(
            jax.ShapeDtypeStruct((OB, C, BT), BF),
            jax.ShapeDtypeStruct((1, 128), F32),
            jax.ShapeDtypeStruct((1, 128), F32),
        ),
        in_specs=[hbm] * 11,
        out_specs=(hbm, vmem, vmem),
        scratch_shapes=scratch,
        compiler_params=pltpu.CompilerParams(
            collective_id=0, has_side_effects=True, vmem_limit_bytes=67043328
        ),
        name="regroup_forward",
    )(
        frames, owners, offsets, groups, rewards,
        norm_gain.reshape(D // 128, 128), latent, noise_blocks, embed_weight, mid_weight, head_weight.T,
    )
    return pred, logp[0, :SPD], adv[0, :SPD]


def solution(mesh):
    placed = (
        P("dp"), P("dp"), P("dp"), P("dp"), P("dp", None, None), P("dp", None, None), P("dp"),
        P(), P(), P(None, "mp"), P("mp", None),
    )
    return jax.shard_map(
        local,
        mesh=mesh,
        in_specs=placed,
        out_specs=(P("dp", None, None), P("dp"), P("dp")),
        check_vma=False,
    )
```

time: 56.2 us -> 40.9 us (0.73)
  Pallas kernels: 45.9 us -> 37.2 us
  local copies, waits for them, and re-layouts: 9.32 us -> 2.89 us
    pallas_call x1, Pallas kernels: 45.9 us -> 37.2 us  [local(): pl.pallas_call(kernel, out_shape=(jax.ShapeDtypeStruct((OB, C, BT), BF),...]
    unnamed x20 -> x1, local copies, waits for them, and re-layouts: 8.8 us -> 1.69 us
    squeeze x1, local copies, waits for them, and re-layouts: 0.52 us -> 1.2 us  [local(): return (pred, logp[0, :SPD], adv[0, :SPD])]
where the time goes in v2:
time: 40.9 us; the launch traced here: 40.8 us
  Pallas kernels  37.2 us (91%)
  local copies, waits for them, and re-layouts  2.89 us (7%)
  between operations  0.64 us (2%)
    pallas_call x1, Pallas kernels, local(): pl.pallas_call(kernel, out_shape=(jax.ShapeDtypeStruct((OB, C, BT), BF),...  37.2 us
    unnamed x1, local copies, waits for them, and re-layouts  1.69 us
    squeeze x1, local copies, waits for them, and re-layouts, local(): return (pred, logp[0, :SPD], adv[0, :SPD])  1.2 us

profile of v2, /device:TPU:1, one launch (start us, length us, event | category | flops | bytes accessed | tf_op | source)
XLA Modules:
  0.0 40.8 jit_solution(15012121768652445701)
XLA Ops:
  0.6 37.2 %regroup_forward.1 = (bf16[18,64,128]{2,1,0:T(8,128)(2,1)}, f32[1,128]{1,0:T(1,128)}, f32[1,128]{1,0:T(1,128)}) custom-call(s32[6]{0:T(128)} %frames_h.1, s32[30]{0:T(128)} %owners_h.1, s32[30]{0:T(128)} %offsets_h.1, s32[6]{0:T(128)} %groups_h.1, f32[6]{0:T(128)} %rewards_h.1, f32[24,128]{1,0:T(8,128)} %bitcast.7, bf16[30,64,128]{2,1,0:T(8,128)(2,1)} %latent_h.1, ...), custom_call_target="tpu_custom_call" | custom-call | tf_op jit(solution)/shard_map/regroup_forward/pallas_call | solution.py:336
  37.9 1.2 %slice_bitcast_fusion = (f32[6]{0:T(128)}, f32[6]{0:T(128)}) fusion(f32[1,128]{1,0:T(1,128)} %get-tuple-element.8, f32[1,128]{1,0:T(1,128)} %get-tuple-element.7), kind=kLoop, calls=%fused_computation | loop fusion | bytes 96 | tf_op jit(solution)/shard_map/squeeze | solution.py:354
  39.1 1.7 %copy.15 = bf16[18,64,128]{2,1,0:T(8,128)(2,1)} copy(bf16[18,64,128]{2,1,0:T(8,128)(2,1)} %get-tuple-element.14) | data formatting | bytes 589824

commit v3 on v2

v3 whole, which is shorter than its diff:
```python
import functools

import jax
import jax.numpy as jnp
from jax import lax
from jax.experimental import pallas as pl
from jax.experimental.pallas import tpu as pltpu
from jax.sharding import PartitionSpec as P

MESH = pl.DeviceIdType.MESH
D = 3072
C = 64
BT = 128
MAXB = 5
SPD = 6
SLOTS = 30
OB = 18
NY, NZ, NC = 4, 8, 2
NDP = NY * NZ * NC
NMP = 4
F = D // NMP
Q = C // NMP
HQ = Q // 2
MCH = 4
MROWS = D // MCH
RB = 128
CHUNKS = 6
CS = SLOTS // CHUNKS
OPEN = 3
SENDS = {
    1: (), 2: (), 3: ((0, 0, 3),), 4: ((0, 3, 1),), 5: ((0, 4, 1),), 6: ((0, 5, 1), (1, 0, 3), (1, 3, 3)),
}
SHARES = tuple(sorted(s for sends in SENDS.values() for s in sends))
BF = jnp.bfloat16
F32 = jnp.float32


def far(k):
    z, y = (k // NC) % NZ, k // (NC * NZ)
    return min(z, NZ - z) + min(y, NY - y)


SHIFTS = sorted(range(1, NDP), key=far, reverse=True)


def peer_of(k):
    return lax.rem(lax.axis_index("dp") + k, NDP)


def kernel(
    frames_h, owners_h, offsets_h, groups_h, rewards_h,
    gain_h, latent_h, noise_h, embed_h, mid_h, head_h,
    pred_o, logp_o, adv_o,
    frames, owners, offsets, groups, rewards,
    ev, gv, mv, lat, noi, av, lw, ht, hb, act0, act1, xs, xr, predb, pay, rcv0, rcv1, rows,
    izt, fzt, itab, ftab, stab, invv, invs, idxv, idxs, ext, exr, err,
    in_sem, s_sem, m_sem, loc_sem, xs_send, xs_recv, z_send, z_recv, meta_send, meta_recv, a2a_send, a2a_recv,
    ag_send, ag_recv, ex_send, ex_recv,
):
    me = lax.axis_index("dp")
    j = lax.axis_index("mp")
    barrier = pltpu.get_barrier_semaphore()

    c_e = pltpu.make_async_copy(embed_h, ev, in_sem.at[0])
    c_g = pltpu.make_async_copy(gain_h, gv, in_sem.at[1])
    c_h = pltpu.make_async_copy(head_h, ht, in_sem.at[2])
    c_l = pltpu.make_async_copy(latent_h, lat, in_sem.at[3])
    c_n = pltpu.make_async_copy(noise_h.at[:, pl.ds(pl.multiple_of(j * Q, Q), Q), :], noi, in_sem.at[4])
    c_m = [
        pltpu.make_async_copy(mid_h.at[pl.ds(k * MROWS, MROWS), :], mv.at[pl.ds(k * MROWS, MROWS), :], m_sem.at[k])
        for k in range(MCH)
    ]
    c_s = [
        pltpu.make_async_copy(src, dst, s_sem.at[k])
        for k, (src, dst) in enumerate(
            ((frames_h, frames), (owners_h, owners), (offsets_h, offsets), (groups_h, groups), (rewards_h, rewards))
        )
    ]
    c_e.start()
    c_g.start()
    c_l.start()
    for c in c_m:
        c.start()
    for c in c_s:
        c.start()

    for k in SHIFTS:
        pl.semaphore_signal(barrier, inc=1, device_id=(peer_of(k), j), device_id_type=MESH)
    for d in range(1, NMP):
        pl.semaphore_signal(barrier, inc=1, device_id=(me, (j + d) % NMP), device_id_type=MESH)

    c_h.start()
    c_n.start()

    lane = lax.broadcasted_iota(jnp.int32, (8, 128), 1)
    sub = lax.broadcasted_iota(jnp.int32, (8, 128), 0)
    zi = (me // NC) % NZ
    yc = (me // (NZ * NC)) * NC + me % NC
    with jax.named_scope("index"):
        for c in c_s:
            c.wait()
        inv = jnp.zeros((8, 128), jnp.int32)
        off = jnp.full((8, 128), -1, jnp.int32)
        counts = jnp.ones((8, 128), jnp.int32)
        fm = jnp.zeros((8, 128), F32)
        gown = jnp.full((8, 128), -1, jnp.int32)
        own = jnp.zeros((8, 128), F32)
        for s in range(SPD):
            n = (frames[s] - 1) // 32 + 1
            counts = jnp.where(sub == s, n, counts)
            for k in range(MAXB):
                slot = s * MAXB + k
                hit = (lane == owners[slot]) & (k < n)
                inv = jnp.where(hit, slot, inv)
                off = jnp.where(hit, offsets[slot], off)
            off = jnp.where(lane == NDP + s, groups[s], off)
            fm = jnp.where(lane == NDP + s, rewards[s], fm)
            gown = jnp.where(sub == s, groups[s], gown)
            own = jnp.where(sub == s, rewards[s], own)
        off = jnp.where(lane >= NDP + SPD, -2, off)
        invv[...] = inv
        izt[zi] = off[0:1, :]
        fzt[zi] = fm[0:1, :]
        c_inv = pltpu.make_async_copy(invv, invs, loc_sem.at[0])
        c_inv.start()

    def pair(p):
        return jnp.concatenate([lat[2 * p], lat[2 * p + 1]], axis=1)

    def stack(x):
        return jnp.concatenate([x, x, x, x], axis=0)

    with jax.named_scope("norm"):
        c_e.wait()
        c_g.wait()
        for k in range(D // 128):
            cols = pl.ds(k * 128, 128)
            eg = ev[:, cols].astype(F32) * gv[k : k + 1, :]
            hi = eg.astype(BF)
            av[0:C, cols] = hi
            av[C : 2 * C, cols] = (eg - hi.astype(F32)).astype(BF)
        gram = jnp.zeros((C, 2 * C), F32)
        for k in range(2):
            e = ev[:, pl.ds(k * (D // 2), D // 2)]
            gram = gram + lax.dot_general(
                e, jnp.concatenate([e, e], axis=0), (((1,), (1,)), ((), ())), preferred_element_type=F32
            )
        g1 = gram.astype(BF).astype(F32)
        g2 = (gram - g1).astype(BF).astype(F32)
        g3 = gram - g1 - g2
        gl = lax.broadcasted_iota(jnp.int32, (C, 2 * C), 1)
        gparts = jnp.concatenate([jnp.where(gl < C, g1, g2), jnp.where(gl < C, g3, 0.0)], axis=1).astype(BF)
        c_l.wait()
        for p in range(SLOTS // 2):
            x = pair(p)
            gx = jnp.dot(gparts, stack(x), preferred_element_type=F32)
            sq = jnp.sum(x.astype(F32) * gx, axis=0, keepdims=True)
            hb[p] = 0.5 * lax.rsqrt(sq * (1.0 / D) + 0.25)

    with jax.named_scope("fold"):
        w = jnp.zeros((2 * C, F), F32)
        for k in range(MCH):
            c_m[k].wait()
            ks = pl.ds(k * MROWS, MROWS)
            w = w + jnp.dot(av[:, ks], mv[ks, :], preferred_element_type=F32)
        w = w[0:C, :] + w[C : 2 * C, :]
        whi = w.astype(BF).astype(F32)
        wst = jnp.concatenate([whi, w - whi], axis=0)
        lw[:, 0 : 2 * C] = jnp.transpose(wst).astype(BF)
        lw[:, 2 * C : 4 * C] = jnp.zeros((F, 2 * C), BF)
        c_h.wait()

    def xcopy(h, g, n, d):
        to = (j + d) % NMP
        sl = pl.ds(g * CS, n * CS)
        return pltpu.make_async_remote_copy(
            src_ref=xs.at[h, to, sl], dst_ref=xr.at[h, d - 1, sl],
            send_sem=xs_send.at[h, g, d - 1], recv_sem=xs_recv.at[h, g, d - 1],
            device_id=(me, to), device_id_type=MESH,
        )

    def z_copies(k):
        to = (me // (NZ * NC)) * (NZ * NC) + lax.rem(zi + k, NZ) * NC + me % NC
        return [
            pltpu.make_async_remote_copy(
                src_ref=t.at[zi], dst_ref=t.at[zi], send_sem=z_send.at[i], recv_sem=z_recv.at[i],
                device_id=(to, j), device_id_type=MESH,
            )
            for i, t in enumerate((izt, fzt))
        ]

    def yc_copies(k):
        q = lax.rem(yc + k, NY * NC)
        to = (q // NC) * (NZ * NC) + zi * NC + q % NC
        return [
            pltpu.make_async_remote_copy(
                src_ref=t, dst_ref=tab.at[pl.ds(yc * NZ, NZ)], send_sem=meta_send.at[i], recv_sem=meta_recv.at[i],
                device_id=(to, j), device_id_type=MESH,
            )
            for i, (t, tab) in enumerate(((izt, itab), (fzt, ftab)))
        ]

    def all_of(ref, n, send, recv):
        return pltpu.make_async_remote_copy(
            src_ref=ref.at[pl.ds(0, n)], dst_ref=ref.at[pl.ds(0, n)], send_sem=send, recv_sem=recv,
            device_id=(me, (j + 1) % NMP), device_id_type=MESH,
        )

    acts = (act0, act1)
    rcvs = (rcv0, rcv1)

    def hidden(p, act):
        x4 = stack(pair(p))
        half = hb[p]
        for b in range(F // RB):
            rs = pl.ds(b * RB, RB)
            h = jnp.dot(lw[rs, :], x4, preferred_element_type=F32) * half
            act[rs, :] = (h + h * jnp.tanh(h)).astype(BF)

    def head(p, act):
        vel = jnp.dot(ht[...], act[...], preferred_element_type=F32).astype(BF)
        for q in range(NMP):
            for h in range(2):
                rs = slice(q * Q + h * HQ, q * Q + (h + 1) * HQ)
                xs[h, q, 2 * p] = vel[rs, 0:BT]
                xs[h, q, 2 * p + 1] = vel[rs, BT : 2 * BT]

    with jax.named_scope("forward"):
        done = 0
        hidden(0, act0)
        for p in range(SLOTS // 2):
            if p + 1 < SLOTS // 2:
                hidden(p + 1, acts[(p + 1) % 2])
            head(p, acts[p % 2])
            while (done + 1) * CS <= 2 * p + 2:
                done += 1
                if done == OPEN:
                    pl.semaphore_wait(barrier, NDP - 1 + NMP - 1)
                    for k in range(1, NZ):
                        for c in z_copies(k):
                            c.start()
                for h, g, n in SENDS[done]:
                    for d in (2, 1, 3):
                        xcopy(h, g, n, d).start()

    with jax.named_scope("meta"):
        all_of(izt, NZ - 1, z_send.at[0], z_recv.at[0]).wait_recv()
        all_of(fzt, NZ - 1, z_send.at[1], z_recv.at[1]).wait_recv()
        for k in range(1, NY * NC):
            for c in yc_copies(k):
                c.start()
        itab[pl.ds(yc * NZ, NZ)] = izt[...]
        ftab[pl.ds(yc * NZ, NZ)] = fzt[...]
        c_n.wait()

    def settle(h):
        for share in SHARES:
            if share[0] != h:
                continue
            for d in range(1, NMP):
                xcopy(*share, d).wait_recv()
            for s in range(share[1], share[1] + share[2]):
                n = (frames[s] - 1) // 32 + 1
                acc = jnp.zeros((HQ, BT), F32)
                for k in range(MAXB):
                    slot = s * MAXB + k
                    v = xs[h, j, slot].astype(F32) + xr[h, 0, slot].astype(F32)
                    v = v + (xr[h, 1, slot].astype(F32) + xr[h, 2, slot].astype(F32))
                    predb[h, slot] = v.astype(BF)
                    dlt = noi[slot, h * HQ : (h + 1) * HQ, :].astype(F32) + v
                    acc = acc + jnp.where(k < n, dlt * dlt, 0.0)
                err[h, s] = jnp.sum(acc, axis=0, keepdims=True)

    def send_blocks(h):
        for o in range(NDP):
            pay[h, o] = predb[h, invs[0, o]]
        for k in SHIFTS:
            p = peer_of(k)
            pltpu.make_async_remote_copy(
                src_ref=pay.at[h, p], dst_ref=rcvs[h].at[me], send_sem=a2a_send.at[h], recv_sem=a2a_recv.at[h],
                device_id=(p, j), device_id_type=MESH,
            ).start()
        rcvs[h][me] = pay[h, me]

    for h in range(2):
        with jax.named_scope("settle%d" % h):
            settle(h)
            if h == 0:
                c_inv.wait()
        with jax.named_scope("send_block%d" % h):
            send_blocks(h)

    et = jnp.zeros((8, 128), F32)
    for s in range(SPD):
        et = jnp.where(sub == s, err[0, s] + err[1, s], et)
    ext[...] = et
    ex = [
        pltpu.make_async_remote_copy(
            src_ref=ext, dst_ref=exr.at[d - 1], send_sem=ex_send.at[d - 1], recv_sem=ex_recv.at[d - 1],
            device_id=(me, (j + d) % NMP), device_id_type=MESH,
        )
        for d in range(1, NMP)
    ]
    for c in ex:
        c.start()

    with jax.named_scope("tables"):
        all_of(itab, NDP - NZ, meta_send.at[0], meta_recv.at[0]).wait_recv()
        all_of(ftab, NDP - NZ, meta_send.at[1], meta_recv.at[1]).wait_recv()
        c_tab = pltpu.make_async_copy(itab, stab, loc_sem.at[1])
        c_tab.start()

        def prompt(s, carry):
            a, b = carry
            hit = gown == itab[s]
            r = jnp.where(hit & (lane >= NDP), jnp.broadcast_to(ftab[s], (8, 128)), 0.0)
            return a + r, b + r * r

        zero = jnp.zeros((8, 128), F32)
        gsum, gsq = lax.fori_loop(0, NDP, prompt, (zero, zero))
        mean = jnp.sum(gsum, axis=1, keepdims=True) * (1.0 / 12.0)
        var = jnp.sum(gsq, axis=1, keepdims=True) * (1.0 / 12.0) - mean * mean
        adv = (own - mean) / jnp.sqrt(var + 0.25)
        adv_o[...] = jnp.sum(jnp.where(lane == sub, adv, 0.0), axis=0, keepdims=True)
        c_tab.wait()
        idx = jnp.zeros((8, 128), jnp.int32)
        for s in range(NDP):
            src = (s // NZ // NC) * (NZ * NC) + (s % NZ) * NC + (s // NZ) % NC
            idx = jnp.where(lane == stab[s, 0, me], src, idx)
        idxv[...] = idx
        c_idx = pltpu.make_async_copy(idxv, idxs, loc_sem.at[2])
        c_idx.start()
        c_idx.wait()

    def gather_copy(h, d):
        return pltpu.make_async_remote_copy(
            src_ref=rows.at[h], dst_ref=pred_o.at[:, pl.ds(pl.multiple_of(j * Q + h * HQ, HQ), HQ), :],
            send_sem=ag_send.at[h, d - 1], recv_sem=ag_recv.at[h, d - 1],
            device_id=(me, (j + d) % NMP), device_id_type=MESH,
        )

    for h in range(2):
        with jax.named_scope("a2a_wait%d" % h):
            all_of(rcvs[h], NDP - 1, a2a_send.at[h], a2a_recv.at[h]).wait_recv()
        for r in range(OB):
            block = rcvs[h][idxs[0, r]]
            rows[h, r] = block
            pred_o[r, pl.ds(pl.multiple_of(j * Q + h * HQ, HQ), HQ), :] = block
        for d in (2, 1, 3):
            gather_copy(h, d).start()
        if h == 0:
            for c in ex:
                c.wait_recv()
            tot = jnp.sum(ext[...] + exr[0] + (exr[1] + exr[2]), axis=1, keepdims=True)
            lp = -0.5 * tot / (counts * (BT * C)).astype(F32)
            logp_o[...] = jnp.sum(jnp.where(lane == sub, lp, 0.0), axis=0, keepdims=True)

    with jax.named_scope("final_wait"):
        all_of(izt, NZ - 1, z_send.at[0], z_recv.at[0]).wait_send()
        all_of(fzt, NZ - 1, z_send.at[1], z_recv.at[1]).wait_send()
        all_of(itab, NDP - NZ, meta_send.at[0], meta_recv.at[0]).wait_send()
        all_of(ftab, NDP - NZ, meta_send.at[1], meta_recv.at[1]).wait_send()
        for share in SHARES:
            for d in range(1, NMP):
                xcopy(*share, d).wait_send()
        for c in ex:
            c.wait_send()
        for h in range(2):
            all_of(rcvs[h], NDP - 1, a2a_send.at[h], a2a_recv.at[h]).wait_send()
            for d in range(1, NMP):
                gather_copy(h, d).wait()


def local(
    frames, owners, offsets, groups, latent, noise_blocks, rewards, embed_weight, norm_gain, mid_weight, head_weight
):
    hbm = pl.BlockSpec(memory_space=pl.ANY)
    vmem = pl.BlockSpec(memory_space=pltpu.VMEM)
    dma = pltpu.SemaphoreType.DMA
    V = pltpu.VMEM
    S = pltpu.SMEM
    scratch = [
        S((SPD,), jnp.int32), S((SLOTS,), jnp.int32), S((SLOTS,), jnp.int32), S((SPD,), jnp.int32), S((SPD,), F32),
        V((C, D), BF), V((D // 128, 128), F32), V((D, F), BF),
        V((SLOTS, C, BT), BF), V((SLOTS, Q, BT), BF),
        V((2 * C, D), BF), V((F, 4 * C), BF), V((C, F), BF),
        V((SLOTS // 2, 1, 2 * BT), F32), V((F, 2 * BT), BF), V((F, 2 * BT), BF),
        V((2, NMP, SLOTS, HQ, BT), BF), V((2, NMP - 1, SLOTS, HQ, BT), BF),
        V((2, SLOTS, HQ, BT), BF), V((2, NDP, HQ, BT), BF), V((NDP, HQ, BT), BF), V((NDP, HQ, BT), BF), V((2, OB, HQ, BT), BF),
        V((NZ, 1, 128), jnp.int32), V((NZ, 1, 128), F32), V((NDP, 1, 128), jnp.int32), V((NDP, 1, 128), F32),
        pltpu.SMEM((NDP, 1, 128), jnp.int32),
        V((8, 128), jnp.int32), pltpu.SMEM((8, 128), jnp.int32),
        V((8, 128), jnp.int32), pltpu.SMEM((8, 128), jnp.int32),
        V((8, 128), F32), V((NMP - 1, 8, 128), F32), V((2, SPD, 1, 128), F32),
        dma((5,)), dma((5,)), dma((MCH,)), dma((3,)),
        dma((2, CHUNKS, NMP - 1)), dma((2, CHUNKS, NMP - 1)),
        dma((2,)), dma((2,)), dma((2,)), dma((2,)), dma((2,)), dma((2,)),
        dma((2, NMP - 1)), dma((2, NMP - 1)), dma((NMP - 1,)), dma((NMP - 1,)),
    ]
    pred, logp, adv = pl.pallas_call(
        kernel,
        out_shape=(
            jax.ShapeDtypeStruct((OB, C, BT), BF),
            jax.ShapeDtypeStruct((1, 128), F32),
            jax.ShapeDtypeStruct((1, 128), F32),
        ),
        in_specs=[hbm] * 11,
        out_specs=(vmem, vmem, vmem),
        scratch_shapes=scratch,
        compiler_params=pltpu.CompilerParams(
            collective_id=0, has_side_effects=True, vmem_limit_bytes=48 * 1024 * 1024
        ),
        name="regroup_forward",
    )(
        *(
            pltpu.with_memory_space_constraint(a, pltpu.HBM)
            for a in (
                frames, owners, offsets, groups, rewards,
                norm_gain.reshape(D // 128, 128), latent, noise_blocks, embed_weight, mid_weight, head_weight.T,
            )
        )
    )
    return pred, logp[0, :SPD], adv[0, :SPD]


def solution(mesh):
    placed = (
        P("dp"), P("dp"), P("dp"), P("dp"), P("dp", None, None), P("dp", None, None), P("dp"),
        P(), P(), P(None, "mp"), P("mp", None),
    )
    return jax.shard_map(
        local,
        mesh=mesh,
        in_specs=placed,
        out_specs=(P("dp", None, None), P("dp"), P("dp")),
        check_vma=False,
    )
```

time: 40.9 us -> 34.1 us (0.83)
  Pallas kernels: 37.2 us -> 32.2 us
  local copies, waits for them, and re-layouts: 2.89 us -> 1.23 us
    pallas_call x1, Pallas kernels: 37.2 us -> 32.2 us  [local(): pl.pallas_call(kernel, out_shape=(jax.ShapeDtypeStruct((OB, C, BT), BF),...]
    unnamed x1, local copies, waits for them, and re-layouts: 1.69 us -> 0.71 us
    squeeze x1, local copies, waits for them, and re-layouts: 1.2 us -> 0.52 us  [local(): return (pred, logp[0, :SPD], adv[0, :SPD])]
where the time goes in v3:
time: 34.1 us
  Pallas kernels  32.2 us (94%)
  local copies, waits for them, and re-layouts  1.23 us (4%)
  between operations  0.64 us (2%)
    pallas_call x1, Pallas kernels, local(): pl.pallas_call(kernel, out_shape=(jax.ShapeDtypeStruct((OB, C, BT), BF),...  32.2 us
    unnamed x1, local copies, waits for them, and re-layouts  0.71 us

profile of v3, /device:TPU:1, one launch (start us, length us, event | category | flops | bytes accessed | tf_op | source)
XLA Modules:
  0.0 34.1 jit_solution(18110898549266511844)
XLA Ops:
  0.6 32.2 %regroup_forward.1 = (bf16[18,64,128]{2,1,0:T(8,128)(2,1)S(1)}, f32[1,128]{1,0:T(1,128)S(1)}, f32[1,128]{1,0:T(1,128)S(1)}) custom-call(s32[6]{0:T(128)} %frames_h.1, s32[30]{0:T(128)} %owners_h.1, s32[30]{0:T(128)} %offsets_h.1, s32[6]{0:T(128)} %groups_h.1, f32[6]{0:T(128)} %rewards_h.1, f32[24,128]{1,0:T(8,128)} %bitcast.7, ...), custom_call_target="tpu_custom_call" | custom-call | tf_op jit(solution)/shard_map/regroup_forward/pallas_call | solution.py:400
  32.8 0.5 %slice_bitcast_fusion = (f32[6]{0:T(128)}, f32[6]{0:T(128)}) fusion(f32[1,128]{1,0:T(1,128)S(1)} %get-tuple-element.8, f32[1,128]{1,0:T(1,128)S(1)} %get-tuple-element.7), kind=kLoop, calls=%fused_computation | loop fusion | bytes 96 | tf_op jit(solution)/shard_map/squeeze | solution.py:423
  33.4 0.7 %copy.15 = bf16[18,64,128]{2,1,0:T(8,128)(2,1)} copy(bf16[18,64,128]{2,1,0:T(8,128)(2,1)S(1)} %get-tuple-element.14) | data formatting | bytes 589824

commit v4 on v3

--- a/solution.py
+++ b/solution.py
@@ -22,15 +22,14 @@
 Q = C // NMP
 HQ = Q // 2
 MCH = 4
+MSTEP = 6
+PAIRS = SLOTS // 2
 MROWS = D // MCH
-RB = 128
-CHUNKS = 6
+RB = 256
+CHUNKS = 5
 CS = SLOTS // CHUNKS
-OPEN = 3
-SENDS = {
-    1: (), 2: (), 3: ((0, 0, 3),), 4: ((0, 3, 1),), 5: ((0, 4, 1),), 6: ((0, 5, 1), (1, 0, 3), (1, 3, 3)),
-}
-SHARES = tuple(sorted(s for sends in SENDS.values() for s in sends))
+OPEN = 2
+SHARES = ((0, 0, OPEN),) + tuple((0, g, 1) for g in range(OPEN, CHUNKS)) + ((1, 0, 3), (1, 3, 2))
 BF = jnp.bfloat16
 F32 = jnp.float32
 
@@ -52,7 +51,7 @@
     gain_h, latent_h, noise_h, embed_h, mid_h, head_h,
     pred_o, logp_o, adv_o,
     frames, owners, offsets, groups, rewards,
-    ev, gv, mv, lat, noi, av, lw, ht, hb, act0, act1, xs, xr, predb, pay, rcv0, rcv1, rows,
+    ev, gv, mv, lat, noi, av, lw, ht, hb, act0, act1, act2, xs, xr, predb, pay, rcv0, rcv1, rows,
     izt, fzt, itab, ftab, stab, invv, invs, idxv, idxs, ext, exr, err,
     in_sem, s_sem, m_sem, loc_sem, xs_send, xs_recv, z_send, z_recv, meta_send, meta_recv, a2a_send, a2a_recv,
     ag_send, ag_recv, ex_send, ex_recv,
@@ -79,16 +78,15 @@
     c_e.start()
     c_g.start()
     c_l.start()
-    for c in c_m:
-        c.start()
     for c in c_s:
         c.start()
 
-    for k in SHIFTS:
-        pl.semaphore_signal(barrier, inc=1, device_id=(peer_of(k), j), device_id_type=MESH)
     for d in range(1, NMP):
         pl.semaphore_signal(barrier, inc=1, device_id=(me, (j + d) % NMP), device_id_type=MESH)
-
+    for i, k in enumerate(SHIFTS):
+        pl.semaphore_signal(barrier, inc=1, device_id=(peer_of(k), j), device_id_type=MESH)
+        if i % MSTEP == MSTEP - 1 and i // MSTEP < MCH:
+            c_m[i // MSTEP].start()
     c_h.start()
     c_n.start()
 
@@ -159,15 +157,15 @@
 
     with jax.named_scope("fold"):
         w = jnp.zeros((2 * C, F), F32)
-        for k in range(MCH):
-            c_m[k].wait()
-            ks = pl.ds(k * MROWS, MROWS)
+        for k in range(2):
+            for c in c_m[k * (MCH // 2) : (k + 1) * (MCH // 2)]:
+                c.wait()
+            ks = pl.ds(k * (D // 2), D // 2)
             w = w + jnp.dot(av[:, ks], mv[ks, :], preferred_element_type=F32)
         w = w[0:C, :] + w[C : 2 * C, :]
         whi = w.astype(BF).astype(F32)
         wst = jnp.concatenate([whi, w - whi], axis=0)
-        lw[:, 0 : 2 * C] = jnp.transpose(wst).astype(BF)
-        lw[:, 2 * C : 4 * C] = jnp.zeros((F, 2 * C), BF)
+        lw[...] = jnp.transpose(wst).astype(BF)
         c_h.wait()
 
     def xcopy(h, g, n, d):
@@ -206,15 +204,16 @@
             device_id=(me, (j + 1) % NMP), device_id_type=MESH,
         )
 
-    acts = (act0, act1)
+    acts = (act0, act1, act2)
     rcvs = (rcv0, rcv1)
 
     def hidden(p, act):
-        x4 = stack(pair(p))
+        x = pair(p)
+        x2 = jnp.concatenate([x, x], axis=0)
         half = hb[p]
         for b in range(F // RB):
             rs = pl.ds(b * RB, RB)
-            h = jnp.dot(lw[rs, :], x4, preferred_element_type=F32) * half
+            h = jnp.dot(lw[rs, :], x2, preferred_element_type=F32) * half
             act[rs, :] = (h + h * jnp.tanh(h)).astype(BF)
 
     def head(p, act):
@@ -226,22 +225,24 @@
                 xs[h, q, 2 * p + 1] = vel[rs, BT : 2 * BT]
 
     with jax.named_scope("forward"):
-        done = 0
         hidden(0, act0)
-        for p in range(SLOTS // 2):
-            if p + 1 < SLOTS // 2:
-                hidden(p + 1, acts[(p + 1) % 2])
-            head(p, acts[p % 2])
-            while (done + 1) * CS <= 2 * p + 2:
-                done += 1
+        for p in range(PAIRS):
+            if p + 1 < PAIRS:
+                hidden(p + 1, acts[(p + 1) % len(acts)])
+            head(p, acts[p % len(acts)])
+            done = (2 * p + 2) // CS
+            if (2 * p + 2) % CS == 0 and done >= OPEN:
                 if done == OPEN:
                     pl.semaphore_wait(barrier, NDP - 1 + NMP - 1)
                     for k in range(1, NZ):
                         for c in z_copies(k):
                             c.start()
-                for h, g, n in SENDS[done]:
-                    for d in (2, 1, 3):
-                        xcopy(h, g, n, d).start()
+                for d in (2, 1, 3):
+                    xcopy(*SHARES[done - OPEN], d).start()
+        for share in SHARES:
+            if share[0] == 1:
+                for d in (2, 1, 3):
+                    xcopy(*share, d).start()
 
     with jax.named_scope("meta"):
         all_of(izt, NZ - 1, z_send.at[0], z_recv.at[0]).wait_recv()
@@ -259,17 +260,12 @@
                 continue
             for d in range(1, NMP):
                 xcopy(*share, d).wait_recv()
-            for s in range(share[1], share[1] + share[2]):
-                n = (frames[s] - 1) // 32 + 1
-                acc = jnp.zeros((HQ, BT), F32)
-                for k in range(MAXB):
-                    slot = s * MAXB + k
-                    v = xs[h, j, slot].astype(F32) + xr[h, 0, slot].astype(F32)
-                    v = v + (xr[h, 1, slot].astype(F32) + xr[h, 2, slot].astype(F32))
-                    predb[h, slot] = v.astype(BF)
-                    dlt = noi[slot, h * HQ : (h + 1) * HQ, :].astype(F32) + v
-                    acc = acc + jnp.where(k < n, dlt * dlt, 0.0)
-                err[h, s] = jnp.sum(acc, axis=0, keepdims=True)
+            for slot in range(share[1] * CS, (share[1] + share[2]) * CS):
+                v = xs[h, j, slot].astype(F32) + xr[h, 0, slot].astype(F32)
+                v = v + (xr[h, 1, slot].astype(F32) + xr[h, 2, slot].astype(F32))
+                predb[h, slot] = v.astype(BF)
+                dlt = noi[slot, h * HQ : (h + 1) * HQ, :].astype(F32) + v
+                err[h, slot] = dlt * dlt
 
     def send_blocks(h):
         for o in range(NDP):
@@ -292,7 +288,11 @@
 
     et = jnp.zeros((8, 128), F32)
     for s in range(SPD):
-        et = jnp.where(sub == s, err[0, s] + err[1, s], et)
+        n = (frames[s] - 1) // 32 + 1
+        acc = jnp.zeros((HQ, BT), F32)
+        for k in range(MAXB):
+            acc = acc + jnp.where(k < n, err[0, s * MAXB + k] + err[1, s * MAXB + k], 0.0)
+        et = jnp.where(sub == s, jnp.sum(acc, axis=0, keepdims=True), et)
     ext[...] = et
     ex = [
         pltpu.make_async_remote_copy(
@@ -383,15 +383,15 @@
         S((SPD,), jnp.int32), S((SLOTS,), jnp.int32), S((SLOTS,), jnp.int32), S((SPD,), jnp.int32), S((SPD,), F32),
         V((C, D), BF), V((D // 128, 128), F32), V((D, F), BF),
         V((SLOTS, C, BT), BF), V((SLOTS, Q, BT), BF),
-        V((2 * C, D), BF), V((F, 4 * C), BF), V((C, F), BF),
-        V((SLOTS // 2, 1, 2 * BT), F32), V((F, 2 * BT), BF), V((F, 2 * BT), BF),
+        V((2 * C, D), BF), V((F, 2 * C), BF), V((C, F), BF),
+        V((SLOTS // 2, 1, 2 * BT), F32), V((F, 2 * BT), BF), V((F, 2 * BT), BF), V((F, 2 * BT), BF),
         V((2, NMP, SLOTS, HQ, BT), BF), V((2, NMP - 1, SLOTS, HQ, BT), BF),
         V((2, SLOTS, HQ, BT), BF), V((2, NDP, HQ, BT), BF), V((NDP, HQ, BT), BF), V((NDP, HQ, BT), BF), V((2, OB, HQ, BT), BF),
         V((NZ, 1, 128), jnp.int32), V((NZ, 1, 128), F32), V((NDP, 1, 128), jnp.int32), V((NDP, 1, 128), F32),
         pltpu.SMEM((NDP, 1, 128), jnp.int32),
         V((8, 128), jnp.int32), pltpu.SMEM((8, 128), jnp.int32),
         V((8, 128), jnp.int32), pltpu.SMEM((8, 128), jnp.int32),
-        V((8, 128), F32), V((NMP - 1, 8, 128), F32), V((2, SPD, 1, 128), F32),
+        V((8, 128), F32), V((NMP - 1, 8, 128), F32), V((2, SLOTS, HQ, BT), F32),
         dma((5,)), dma((5,)), dma((MCH,)), dma((3,)),
         dma((2, CHUNKS, NMP - 1)), dma((2, CHUNKS, NMP - 1)),
         dma((2,)), dma((2,)), dma((2,)), dma((2,)), dma((2,)), dma((2,)),

time: 34.1 us -> 33.5 us (0.982)
  Pallas kernels: 32.2 us -> 31.6 us
    pallas_call x1, Pallas kernels: 32.2 us -> 31.6 us  [local(): pl.pallas_call(kernel, out_shape=(jax.ShapeDtypeStruct((OB, C, BT), BF),...]
where the time goes in v4:
time: 33.5 us; the launch traced here: 33.4 us
  Pallas kernels  31.6 us (94%)
  local copies, waits for them, and re-layouts  1.23 us (4%)
  between operations  0.64 us (2%)
    pallas_call x1, Pallas kernels, local(): pl.pallas_call(kernel, out_shape=(jax.ShapeDtypeStruct((OB, C, BT), BF),...  31.6 us
    unnamed x1, local copies, waits for them, and re-layouts  0.71 us

profile of v4, /device:TPU:1, one launch (start us, length us, event | category | flops | bytes accessed | tf_op | source)
XLA Modules:
  0.0 33.4 jit_solution(14570899304680610430)
XLA Ops:
  0.6 31.6 %regroup_forward.1 = (bf16[18,64,128]{2,1,0:T(8,128)(2,1)S(1)}, f32[1,128]{1,0:T(1,128)S(1)}, f32[1,128]{1,0:T(1,128)S(1)}) custom-call(s32[6]{0:T(128)} %frames_h.1, s32[30]{0:T(128)} %owners_h.1, s32[30]{0:T(128)} %offsets_h.1, s32[6]{0:T(128)} %groups_h.1, f32[6]{0:T(128)} %rewards_h.1, f32[24,128]{1,0:T(8,128)} %bitcast.7, ...), custom_call_target="tpu_custom_call" | custom-call | tf_op jit(solution)/shard_map/regroup_forward/pallas_call | solution.py:400
  32.2 0.5 %slice_bitcast_fusion = (f32[6]{0:T(128)}, f32[6]{0:T(128)}) fusion(f32[1,128]{1,0:T(1,128)S(1)} %get-tuple-element.8, f32[1,128]{1,0:T(1,128)S(1)} %get-tuple-element.7), kind=kLoop, calls=%fused_computation | loop fusion | bytes 96 | tf_op jit(solution)/shard_map/squeeze | solution.py:423
  32.7 0.7 %copy.15 = bf16[18,64,128]{2,1,0:T(8,128)(2,1)} copy(bf16[18,64,128]{2,1,0:T(8,128)(2,1)S(1)} %get-tuple-element.14) | data formatting | bytes 589824

commit v5 on v4

--- a/solution.py
+++ b/solution.py
@@ -28,7 +28,7 @@
 RB = 256
 CHUNKS = 5
 CS = SLOTS // CHUNKS
-OPEN = 2
+OPEN = 1
 SHARES = ((0, 0, OPEN),) + tuple((0, g, 1) for g in range(OPEN, CHUNKS)) + ((1, 0, 3), (1, 3, 2))
 BF = jnp.bfloat16
 F32 = jnp.float32

time: 33.5 us -> 33.4 us (level)
  no operation moved by 1% of the time
where the time goes in v5:
time: 33.4 us; the launch traced here: 33.3 us
  Pallas kernels  31.4 us (94%)
  local copies, waits for them, and re-layouts  1.23 us (4%)
  between operations  0.64 us (2%)
    pallas_call x1, Pallas kernels, local(): pl.pallas_call(kernel, out_shape=(jax.ShapeDtypeStruct((OB, C, BT), BF),...  31.4 us
    unnamed x1, local copies, waits for them, and re-layouts  0.71 us

profile of v5, /device:TPU:1, one launch (start us, length us, event | category | flops | bytes accessed | tf_op | source)
XLA Modules:
  0.0 33.3 jit_solution(17362846408243430290)
XLA Ops:
  0.6 31.4 %regroup_forward.1 = (bf16[18,64,128]{2,1,0:T(8,128)(2,1)S(1)}, f32[1,128]{1,0:T(1,128)S(1)}, f32[1,128]{1,0:T(1,128)S(1)}) custom-call(s32[6]{0:T(128)} %frames_h.1, s32[30]{0:T(128)} %owners_h.1, s32[30]{0:T(128)} %offsets_h.1, s32[6]{0:T(128)} %groups_h.1, f32[6]{0:T(128)} %rewards_h.1, f32[24,128]{1,0:T(8,128)} %bitcast.7, ...), custom_call_target="tpu_custom_call" | custom-call | tf_op jit(solution)/shard_map/regroup_forward/pallas_call | solution.py:400
  32.0 0.5 %slice_bitcast_fusion = (f32[6]{0:T(128)}, f32[6]{0:T(128)}) fusion(f32[1,128]{1,0:T(1,128)S(1)} %get-tuple-element.8, f32[1,128]{1,0:T(1,128)S(1)} %get-tuple-element.7), kind=kLoop, calls=%fused_computation | loop fusion | bytes 96 | tf_op jit(solution)/shard_map/squeeze | solution.py:423
  32.6 0.7 %copy.15 = bf16[18,64,128]{2,1,0:T(8,128)(2,1)} copy(bf16[18,64,128]{2,1,0:T(8,128)(2,1)S(1)} %get-tuple-element.14) | data formatting | bytes 589824

commit v6 on v5

--- a/solution.py
+++ b/solution.py
@@ -25,7 +25,7 @@
 MSTEP = 6
 PAIRS = SLOTS // 2
 MROWS = D // MCH
-RB = 256
+RB = 192
 CHUNKS = 5
 CS = SLOTS // CHUNKS
 OPEN = 1

time: 33.4 us -> 33.6 us (level)
  no operation moved by 1% of the time
where the time goes in v6:
time: 33.6 us; the launch traced here: 33.5 us
  Pallas kernels  31.6 us (94%)
  local copies, waits for them, and re-layouts  1.23 us (4%)
  between operations  0.64 us (2%)
    pallas_call x1, Pallas kernels, local(): pl.pallas_call(kernel, out_shape=(jax.ShapeDtypeStruct((OB, C, BT), BF),...  31.6 us
    unnamed x1, local copies, waits for them, and re-layouts  0.71 us

profile of v6, /device:TPU:1, one launch (start us, length us, event | category | flops | bytes accessed | tf_op | source)
XLA Modules:
  0.0 33.5 jit_solution(12199163746800707661)
XLA Ops:
  0.6 31.6 %regroup_forward.1 = (bf16[18,64,128]{2,1,0:T(8,128)(2,1)S(1)}, f32[1,128]{1,0:T(1,128)S(1)}, f32[1,128]{1,0:T(1,128)S(1)}) custom-call(s32[6]{0:T(128)} %frames_h.1, s32[30]{0:T(128)} %owners_h.1, s32[30]{0:T(128)} %offsets_h.1, s32[6]{0:T(128)} %groups_h.1, f32[6]{0:T(128)} %rewards_h.1, f32[24,128]{1,0:T(8,128)} %bitcast.7, ...), custom_call_target="tpu_custom_call" | custom-call | tf_op jit(solution)/shard_map/regroup_forward/pallas_call | solution.py:400
  32.3 0.5 %slice_bitcast_fusion = (f32[6]{0:T(128)}, f32[6]{0:T(128)}) fusion(f32[1,128]{1,0:T(1,128)S(1)} %get-tuple-element.8, f32[1,128]{1,0:T(1,128)S(1)} %get-tuple-element.7), kind=kLoop, calls=%fused_computation | loop fusion | bytes 96 | tf_op jit(solution)/shard_map/squeeze | solution.py:423
  32.8 0.7 %copy.15 = bf16[18,64,128]{2,1,0:T(8,128)(2,1)} copy(bf16[18,64,128]{2,1,0:T(8,128)(2,1)S(1)} %get-tuple-element.14) | data formatting | bytes 589824
